TPU v7x, 128 devices: a whole 4x4x4 slice. The times are simulated.
128 devices in a mesh: blk: 32 (over x_hi, z, y), sub: 4 (over x_lo, core).
Axes of the slice: x: 4 (x_hi: 2, x_lo: 2; x = x_hi * 2 + x_lo), y: 4, z: 4, core: 2. Of those that a mesh axis runs over, the one named last changes fastest.
Arguments:
- integrals: float32 [32, 4, 32, 6144], P('blk', 'sub'), may hold values from -1 to 1
- slot_order: int32 [32, 4, 32], P('blk', 'sub'), may hold values from 0 to 31, each once within a row
- factor_rows: float32 [32, 4, 32, 4096], P(None, 'sub'), may hold values from -1 to 1.5, as said below
- occ_energy: float32 [384], replicated, may hold values from -1.5 to -0.3
- slab_index: int32 [1], replicated, may hold values from 0 to 127
- virt_energy: float32 [2048], replicated, may hold values from 0.1 to 3
Outputs:
- amplitudes: float32 [6144, 6144], P('blk', 'sub')
Inputs may be any that keep to these rules, and one draw needn't show every extreme that they name: `slot_order`: each row of 32 entries holds every number from 0 to 31 once. `factor_rows`: the factor is lower triangular (zero above its diagonal) with diagonal entries between 0.5 and 1.5.
All inputs are finite; a program needn't handle non-finite values.
Results may differ from a plain program's by a relative error of at most 0.0001.
Values sent between devices are 32-bit elements; how exact they have to be, the bound alone decides.
A program may use at most 128 MiB of HBM per device.

v0:
```python
import jax
import jax.numpy as jnp
from jax import lax
from jax.sharding import PartitionSpec as P

NVIRT = 2048
NOCC = 3


PRECISE = lax.Precision.HIGHEST


def canonical_order(integrals, slot_order):
    piece_len = integrals.shape[2]
    places = jnp.arange(piece_len, dtype=jnp.int32)
    onehot = (slot_order[..., None] == places).astype(jnp.float32)
    return jnp.einsum("rscq,rscp->rsqp", onehot, integrals, precision=PRECISE)


def transposed_dot(left, right):
    return lax.dot_general(left, right, (((0,), (0,)), ((), ())), precision=PRECISE)


def after_section(solved, own_rows, rhs_rows, diag_inverse, first, reach):
    round_width = diag_inverse.shape[1]
    pair_cols = solved.shape[2]
    width = reach * round_width
    rows_part = own_rows[:, :, :width]

    def advance(round_id, solved):
        factor_part = lax.dynamic_index_in_dim(rows_part, round_id, 0, keepdims=False)
        known_part = jnp.dot(
            factor_part, solved[:reach].reshape(width, pair_cols), precision=PRECISE
        )
        updated = lax.dynamic_index_in_dim(rhs_rows, round_id, 0, keepdims=False) - known_part
        round_block = lax.all_gather(updated[None], "sub", axis=0, tiled=True).reshape(
            round_width, pair_cols
        )
        inverse = lax.dynamic_index_in_dim(diag_inverse, round_id, 0, keepdims=False)
        solved_round = jnp.dot(inverse, round_block, precision=PRECISE)
        return lax.dynamic_update_index_in_dim(solved, solved_round, round_id, 0)

    return lax.fori_loop(first, reach, advance, solved, unroll=True)


def shards(integrals, slot_order, factor_rows, occ_energy, slab_index, virt_energy):
    canonical = canonical_order(integrals, slot_order)
    local_rhs = lax.all_to_all(canonical, "blk", split_axis=3, concat_axis=0, tiled=True)
    rounds = factor_rows.shape[0]
    piece_len = factor_rows.shape[2]
    sub_count = lax.axis_size("sub")
    round_width = sub_count * piece_len
    pair_cols = local_rhs.shape[3]
    shaped = factor_rows.reshape(rounds, piece_len, rounds, round_width)
    round_ids = jnp.arange(rounds)
    own_diag = shaped[round_ids, :, round_ids, :]
    diag_blocks = lax.all_gather(own_diag[:, None], "sub", axis=1, tiled=True).reshape(
        rounds, round_width, round_width
    )
    identity = jnp.broadcast_to(
        jnp.eye(round_width, dtype=jnp.float32), (rounds, round_width, round_width)
    )
    diag_inverse = jax.scipy.linalg.solve_triangular(diag_blocks, identity, lower=True)
    rhs_rows = local_rhs[:, 0]
    own_rows = factor_rows[:, 0]
    solved_start = jnp.zeros((rounds, round_width, pair_cols), jnp.float32)
    section_count = min(8, rounds)
    per_section = rounds // section_count
    solved = solved_start
    for section_id in range(section_count):
        solved = after_section(
            solved,
            own_rows,
            rhs_rows,
            diag_inverse,
            section_id * per_section,
            (section_id + 1) * per_section,
        )
    sub_index = lax.axis_index("sub")
    total_pairs = pair_cols * lax.axis_size("blk")
    quarter = total_pairs // sub_count
    solved_full = solved.reshape(rounds, sub_count, piece_len, pair_cols)
    own_part = lax.dynamic_index_in_dim(solved_full, sub_index, 1, keepdims=False).reshape(
        rounds * piece_len, pair_cols
    )
    product = transposed_dot(own_part, lax.all_gather(own_part, "blk", axis=1, tiled=True))
    coulomb = lax.psum_scatter(product, "sub", scatter_dimension=1, tiled=True)
    slab_start = slab_index[0] * NOCC
    occ_slab = lax.dynamic_slice_in_dim(occ_energy, slab_start, NOCC)
    pair_energy = jnp.repeat(occ_slab, NVIRT) - jnp.tile(virt_energy, NOCC)
    row_energy = lax.dynamic_slice_in_dim(pair_energy, lax.axis_index("blk") * pair_cols, pair_cols)
    col_energy = lax.dynamic_slice_in_dim(pair_energy, sub_index * quarter, quarter)
    return coulomb / (row_energy[:, None] + col_energy[None, :])


def solution(mesh):
    in_specs = (
        P("blk", "sub", None, None),
        P("blk", "sub", None),
        P(None, "sub", None, None),
        P(),
        P(),
        P(),
    )
    out_specs = P("blk", "sub")
    return jax.shard_map(shards, mesh=mesh, in_specs=in_specs, out_specs=out_specs, check_vma=False)
```

profile of v0, /device:TPU:5, one launch (start us, length us, event | category | flops | bytes accessed | tf_op | source)
XLA Modules:
  0.0 1047.5 jit_solution(18089864629097165901)
XLA Ops:
  6.5 9.5 copy.309
  16.0 13.8 %copy.144 = f32[32,32,32,128]{3,1,2,0:T(8,128)} copy(f32[32,32,32,128]{3,2,1,0:T(8,128)S(1)} %bitcast.879) | data formatting | bytes 33554432 | tf_op jit(solution)/shard_map/reshape | solution.py:54
  29.8 7.2 gather_fusion
  41.8 27.9 %reduce.8 = f32[6144,32]{1,0:T(8,128)S(1)} reduce(f32[6144,1,1,32]{3,2,1,0:T(1,128)} %bitcast.909, f32[]{:T(128)} %broadcast.107), dimensions={1,2}, to_apply=%bitcast.777.reduce_sub_computation | reduce | bytes 1572868
  72.0 10.5 %all-to-all-start = ((f32[32,1,6144]{2,1,0:T(1,128)}), f32[32,1,6144]{2,1,0:T(1,128)S(1)}, u32[]{:S(2)}, u32[]{:S(2)}) async-start(f32[32,1,6144]{2,1,0:T(1,128)} %reshape.582), calls=%async_computation | async-start | bytes 1572864 | tf_op jit(solution)/shard_map/all_to_all | solution.py:48
  84.7 10.1 all-to-all-done
  98.2 6.6 reshape.583
  138.3 7.4 all_gather.103
  147.4 315.4 %custom-call.4 = f32[32,1,128,128]{2,3,1,0:T(8,128)} custom-call(f32[32,1,128,128]{3,2,1,0:T(8,128)S(1)} %bitcast_select_fusion), custom_call_target="InvertDiagBlocksLowerTriangular" | custom-call | tf_op jit(solution)/shard_map/jit(_solve_triangular)/vmap()/triangular_solve | solution.py:63
  506.7 5.6 all-gather.6
  562.5 5.4 all-gather.13
  570.7 5.6 all-gather.14
  579.2 5.4 all-gather.15
  596.5 5.4 all-gather.17
  613.7 5.4 all-gather.19
  622.7 5.9 all-gather.20
  641.1 5.4 all-gather.22
  659.4 5.4 all-gather.24
  668.7 5.6 all-gather.25
  687.6 5.4 all-gather.27
  707.1 5.4 all-gather.29
  738.2 203.6 %all-gather.35.cloned.1.call-done = f32[1024,6144]{0,1:T(8,128)} async-done(((f32[1024,192]{0,1:T(8,128)}), f32[1024,6144]{0,1:T(8,128)}) %all-gather.35.cloned.1.call-update) | async-done | bytes 25165840 | tf_op jit(solution)/shard_map/all_gather | solution.py:86
  941.8 45.4 %fusion.289 = f32[192,6144]{1,0:T(8,128)} fusion(f32[1024,192]{1,0:T(8,128)S(1)} %bitcast.913, f32[1024,6144]{0,1:T(8,128)} %all-gather.35.cloned.1.call-done), kind=kOutput, calls=%fused_computation.328 | convolution fusion | flops 14495514624 | bytes 30670848 | tf_op jit(solution)/shard_map/dot_general | solution.py:21
  989.1 49.0 %reduce-scatter.2.cloned.1.call-done = f32[192,1536]{1,0:T(8,128)} async-done(((f32[192,6144]{1,0:T(8,128)}), f32[192,1536]{1,0:T(8,128)}) %reduce-scatter.2.cloned.1.call-update) | async-done | bytes 1179664 | tf_op jit(solution)/shard_map/reduce_scatter | solution.py:87
  (207 shorter events, 259.9 us)
Async XLA Ops:
  6.5 30.5 %copy-start = (f32[1,1,32,6144]{3,2,1,0:T(8,128)S(1)}, f32[1,1,32,6144]{3,2,1,0:T(8,128)}, u32[]{:S(2)}) copy-start(f32[1,1,32,6144]{3,2,1,0:T(8,128)} %param.6) | copy-start | bytes 2359300
  6.5 139.1 %all-gather.37.cloned.1.call-start = ((), (), s32[]{:S(2)}) async-start(), calls=%async_computation.4 | async-start | bytes 2621440 | tf_op jit(solution)/shard_map/all_gather | solution.py:57
  72.0 22.8 %all-to-all-start = ((f32[32,1,6144]{2,1,0:T(1,128)}), f32[32,1,6144]{2,1,0:T(1,128)S(1)}, u32[]{:S(2)}, u32[]{:S(2)}) async-start(f32[32,1,6144]{2,1,0:T(1,128)} %reshape.582), calls=%async_computation | async-start | bytes 1572864 | tf_op jit(solution)/shard_map/all_to_all | solution.py:48
  82.5 859.3 %all-gather.35.cloned.1.call-start = ((), (), s32[]{:S(2)}) async-start(), calls=%async_computation.2 | async-start | bytes 25952256 | tf_op jit(solution)/shard_map/all_gather | solution.py:86
  107.7 26.3 %copy-start.9 = (f32[1,1,32,1,192]{2,4,3,1,0:T(8,128)S(1)}, f32[1,1,32,1,192]{2,4,3,1,0:T(8,128)}, u32[]{:S(2)}) copy-start(f32[1,1,32,1,192]{2,4,3,1,0:T(8,128)} %get-tuple-element.16) | copy-start | bytes 73732
  107.7 26.4 %copy-start.8 = (f32[1,1,32,1,192]{2,4,3,1,0:T(8,128)S(1)}, f32[1,1,32,1,192]{2,4,3,1,0:T(8,128)}, u32[]{:S(2)}) copy-start(f32[1,1,32,1,192]{2,4,3,1,0:T(8,128)} %get-tuple-element.17) | copy-start | bytes 73732
  107.7 26.5 %copy-start.7 = (f32[1,1,32,1,192]{2,4,3,1,0:T(8,128)S(1)}, f32[1,1,32,1,192]{2,4,3,1,0:T(8,128)}, u32[]{:S(2)}) copy-start(f32[1,1,32,1,192]{2,4,3,1,0:T(8,128)} %get-tuple-element.18) | copy-start | bytes 73732
  107.7 27.2 %copy-start.6 = (f32[1,1,32,1,192]{2,4,3,1,0:T(8,128)S(1)}, f32[1,1,32,1,192]{2,4,3,1,0:T(8,128)}, u32[]{:S(2)}) copy-start(f32[1,1,32,1,192]{2,4,3,1,0:T(8,128)} %get-tuple-element.19) | copy-start | bytes 73732
  107.7 27.8 %copy-start.5 = (f32[1,1,32,1,192]{2,4,3,1,0:T(8,128)S(1)}, f32[1,1,32,1,192]{2,4,3,1,0:T(8,128)}, u32[]{:S(2)}) copy-start(f32[1,1,32,1,192]{2,4,3,1,0:T(8,128)} %get-tuple-element.20) | copy-start | bytes 73732
  107.7 28.5 %copy-start.4 = (f32[1,1,32,1,192]{2,4,3,1,0:T(8,128)S(1)}, f32[1,1,32,1,192]{2,4,3,1,0:T(8,128)}, u32[]{:S(2)}) copy-start(f32[1,1,32,1,192]{2,4,3,1,0:T(8,128)} %get-tuple-element.21) | copy-start | bytes 73732
  107.7 29.2 %copy-start.3 = (f32[1,1,32,1,192]{2,4,3,1,0:T(8,128)S(1)}, f32[1,1,32,1,192]{2,4,3,1,0:T(8,128)}, u32[]{:S(2)}) copy-start(f32[1,1,32,1,192]{2,4,3,1,0:T(8,128)} %get-tuple-element.22) | copy-start | bytes 73732
  107.7 29.9 %copy-start.2 = (f32[1,1,32,1,192]{2,4,3,1,0:T(8,128)S(1)}, f32[1,1,32,1,192]{2,4,3,1,0:T(8,128)}, u32[]{:S(2)}) copy-start(f32[1,1,32,1,192]{2,4,3,1,0:T(8,128)} %get-tuple-element.23) | copy-start | bytes 73732
  128.1 334.7 %copy-start.10 = (f32[128,128]{1,0:T(8,128)S(1)}, f32[128,128]{1,0:T(8,128)}, u32[]{:S(2)}) copy-start(f32[128,128]{1,0:T(8,128)} %fusion.283) | copy-start | bytes 196612
  475.3 29.7 %copy-start.20 = (f32[1,1,32,1,192]{4,2,3,1,0:T(8,128)S(1)}, f32[1,1,32,1,192]{4,2,3,1,0:T(8,128)}, u32[]{:S(2)}) copy-start(f32[1,1,32,1,192]{4,2,3,1,0:T(8,128)} %copy.252) | copy-start | bytes 73732
  475.7 37.0 %copy-start.19 = (f32[1,1,32,1,192]{4,2,3,1,0:T(8,128)S(1)}, f32[1,1,32,1,192]{4,2,3,1,0:T(8,128)}, u32[]{:S(2)}) copy-start(f32[1,1,32,1,192]{4,2,3,1,0:T(8,128)} %copy.253) | copy-start | bytes 73732
  484.1 36.1 %copy-start.18 = (f32[1,1,32,1,192]{4,2,3,1,0:T(8,128)S(1)}, f32[1,1,32,1,192]{4,2,3,1,0:T(8,128)}, u32[]{:S(2)}) copy-start(f32[1,1,32,1,192]{4,2,3,1,0:T(8,128)} %copy.254) | copy-start | bytes 73732
  497.4 30.6 %copy-start.17 = (f32[1,1,32,1,192]{4,2,3,1,0:T(8,128)S(1)}, f32[1,1,32,1,192]{4,2,3,1,0:T(8,128)}, u32[]{:S(2)}) copy-start(f32[1,1,32,1,192]{4,2,3,1,0:T(8,128)} %copy.255) | copy-start | bytes 73732
  505.0 31.0 %copy-start.16 = (f32[1,1,32,1,192]{4,2,3,1,0:T(8,128)S(1)}, f32[1,1,32,1,192]{4,2,3,1,0:T(8,128)}, u32[]{:S(2)}) copy-start(f32[1,1,32,1,192]{4,2,3,1,0:T(8,128)} %copy.256) | copy-start | bytes 73732
  514.4 29.5 %copy-start.15 = (f32[1,1,32,1,192]{4,2,3,1,0:T(8,128)S(1)}, f32[1,1,32,1,192]{4,2,3,1,0:T(8,128)}, u32[]{:S(2)}) copy-start(f32[1,1,32,1,192]{4,2,3,1,0:T(8,128)} %copy.257) | copy-start | bytes 73732
  522.3 29.5 %copy-start.28 = (f32[1,1,32,1,192]{4,2,3,1,0:T(8,128)S(1)}, f32[1,1,32,1,192]{4,2,3,1,0:T(8,128)}, u32[]{:S(2)}) copy-start(f32[1,1,32,1,192]{4,2,3,1,0:T(8,128)} %copy.258) | copy-start | bytes 73732
  551.8 25.0 %copy-start.25 = (f32[1,1,32,1,192]{4,2,3,1,0:T(8,128)S(1)}, f32[1,1,32,1,192]{4,2,3,1,0:T(8,128)}, u32[]{:S(2)}) copy-start(f32[1,1,32,1,192]{4,2,3,1,0:T(8,128)} %copy.261) | copy-start | bytes 73732
  560.0 25.0 %copy-start.14 = (f32[1,1,32,1,192]{4,2,3,1,0:T(8,128)S(1)}, f32[1,1,32,1,192]{4,2,3,1,0:T(8,128)}, u32[]{:S(2)}) copy-start(f32[1,1,32,1,192]{4,2,3,1,0:T(8,128)} %copy.262) | copy-start | bytes 73732
  738.2 299.9 %reduce-scatter.2.cloned.1.call-start = ((), (), s32[]{:S(2)}) async-start(), calls=%async_computation.3 | async-start | bytes 5898240 | tf_op jit(solution)/shard_map/reduce_scatter | solution.py:87
  987.3 53.3 %copy-start.1 = (f32[1,1,32,6144]{3,2,1,0:T(8,128)S(1)}, f32[1,1,32,6144]{3,2,1,0:T(8,128)}, u32[]{:S(2)}) copy-start(f32[1,1,32,6144]{3,2,1,0:T(8,128)} %param.6) | copy-start | bytes 2359300
  (11 other events, 192.1 us)
Sparse Core Ops, SparseCore 0:
  37.1 31.5 all-gather.36
  738.3 203.5 all-gather.34
  987.4 50.6 reduce-scatter.1
where the time goes:
time: 1060 us; the launch traced here: 1050 us
  other arithmetic  354 us (33%)
  waiting for transfers between devices  263 us (25%)
  blocking collectives  176 us (17%)
  matrix products  149 us (14%)
  local copies, waits for them, and re-layouts  79.6 us (8%)
  between operations  15.2 us (1%)
  starting transfers between devices  10.6 us (1%)
    another operation x3, other arithmetic, shards(): jax.scipy.linalg.solve_triangular(diag_blocks, identity, lower=True)  317 us
    all_gather x1, waiting for transfers between devices, shards(): lax.all_gather(own_part, 'blk', axis=1, tiled=True)  204 us
    all_gather x32, blocking collectives, advance(): lax.all_gather(updated[None], 'sub', axis=0, tiled=True)  176 us
    dot_general x31, matrix products, advance(): jnp.dot(factor_part, solved[:reach].reshape(width, pair_cols), precision=...  82.3 us
    unnamed x98, local copies, waits for them, and re-layouts  49.4 us
    reduce_scatter x1, waiting for transfers between devices, shards(): coulomb = lax.psum_scatter(product, 'sub', scatter_dimension=1, tiled=True)  49 us
    dot_general x1, matrix products, transposed_dot(): lax.dot_general(left, right, (((0,), (0,)), ((), ())), precision=PRECISE)  45.4 us
    unnamed x1, other arithmetic  27.9 us
  transfers between devices with their start and end apart: 4, of which 3 were waited for; matrix products, arithmetic and copies ran while one was open for 8% of the time, Pallas kernels for 0%

commit v1 on v0

--- a/solution.py
+++ b/solution.py
@@ -1,13 +1,32 @@
+import functools
+
 import jax
 import jax.numpy as jnp
 from jax import lax
+from jax.experimental import pallas as pl
+from jax.experimental.pallas import tpu as pltpu
 from jax.sharding import PartitionSpec as P
 
 NVIRT = 2048
 NOCC = 3
-
-
 PRECISE = lax.Precision.HIGHEST
+F32 = jnp.float32
+BF16 = jnp.bfloat16
+MESH = pl.DeviceIdType.MESH
+NN = (((1,), (0,)), ((), ()))
+NT = (((1,), (1,)), ((), ()))
+
+
+def split(x):
+    high = x.astype(BF16)
+    return high, (x - high.astype(F32)).astype(BF16)
+
+
+def dot3(a, b, dims):
+    def one(p, q):
+        return lax.dot_general(p, q, dims, preferred_element_type=F32)
+
+    return one(a[0], b[0]) + (one(a[0], b[1]) + one(a[1], b[0]))
 
 
 def canonical_order(integrals, slot_order):
@@ -17,8 +36,217 @@
     return jnp.einsum("rscq,rscp->rsqp", onehot, integrals, precision=PRECISE)
 
 
-def transposed_dot(left, right):
-    return lax.dot_general(left, right, (((0,), (0,)), ((), ())), precision=PRECISE)
+def inverse_of(block):
+    n = block.shape[0]
+    row = lax.broadcasted_iota(jnp.int32, (n, n), 0)
+    col = lax.broadcasted_iota(jnp.int32, (n, n), 1)
+    diag = jnp.sum(jnp.where(row == col, block, 0.0), axis=1, keepdims=True)
+    inv = jnp.where(row == col, 1.0 / diag, 0.0)
+    size = 1
+    while size < n:
+        below = (row // size == col // size + 1) & (row // (2 * size) == col // (2 * size))
+        part = split(jnp.where(below, block, 0.0))
+        now = split(inv)
+        inv = inv - dot3(now, split(dot3(part, now, NN)), NN)
+        size *= 2
+    return inv
+
+
+def inverse_kernel(diag_ref, inv_ref):
+    for k in range(diag_ref.shape[0]):
+        inv_ref[k] = inverse_of(diag_ref[k])
+
+
+def diag_inverses(diag_blocks):
+    rounds, width, _ = diag_blocks.shape
+    batch = 8
+    spec = pl.BlockSpec((batch, width, width), lambda i: (i, 0, 0))
+    return pl.pallas_call(
+        inverse_kernel,
+        grid=(rounds // batch,),
+        in_specs=[spec],
+        out_specs=spec,
+        out_shape=jax.ShapeDtypeStruct(diag_blocks.shape, F32),
+    )(diag_blocks)
+
+
+def gram_kernel(own, out, rowbuf, colbuf, acc, colh, coll, exch, total, final,
+                y_send, y_recv, z_send, z_recv, s_send, s_recv, t_send, t_recv):
+    chunks, rows, depth = own.shape
+    half = 2 * rows
+    blk, sub = lax.axis_index("blk"), lax.axis_index("sub")
+    y, z, xh = blk % 4, (blk // 4) % 4, blk // 16
+    xl, core = sub // 2, sub % 2
+    same = xh == xl
+
+    def y_at(offset):
+        return {"blk": blk - y + (y + offset + 4) % 4, "sub": sub}
+
+    def z_at(offset):
+        return {"blk": blk - 4 * z + 4 * ((z + offset + 4) % 4), "sub": sub}
+
+    swap = {"blk": blk + (1 - 2 * xh) * 16, "sub": sub + (1 - 2 * xl) * 2}
+    mate = {"blk": blk, "sub": sub + 1 - 2 * core}
+
+    barrier = pltpu.get_barrier_semaphore()
+    for who in (y_at(1), y_at(-1), y_at(2), z_at(1), z_at(-1), swap, mate):
+        pl.semaphore_signal(barrier, inc=1, device_id=who, device_id_type=MESH)
+    pl.semaphore_wait(barrier, 7)
+
+    def copy(src, dst, send, recv, who):
+        return pltpu.make_async_remote_copy(
+            src_ref=src, dst_ref=dst, send_sem=send, recv_sem=recv,
+            device_id=who, device_id_type=MESH)
+
+    def y_own(c):
+        for k, offset in enumerate((1, -1)):
+            copy(own.at[c], rowbuf.at[y, c], y_send.at[k, c], y_recv.at[k, c], y_at(offset)).start()
+
+    def z_own(c):
+        @pl.when(same)
+        def _():
+            for k, offset in enumerate((1, -1)):
+                copy(own.at[c], colbuf.at[z, c], z_send.at[k, c], z_recv.at[k, c], z_at(offset)).start()
+
+        @pl.when(jnp.logical_not(same))
+        def _():
+            copy(own.at[c], colbuf.at[z, c], s_send.at[c], s_recv.at[c], swap).wait_recv()
+            for k, offset in enumerate((1, -1)):
+                copy(colbuf.at[z, c], colbuf.at[z, c], z_send.at[k, c], z_recv.at[k, c], z_at(offset)).start()
+
+    def got(buf, recv, send, place, k, c):
+        copy(buf.at[place, c], buf.at[place, c], send.at[k, c], recv.at[k, c], mate).wait_recv()
+
+    def forward(c):
+        odd = c % 2
+        step = 1 - 2 * odd
+        src = (y - step + 4) % 4
+        got(rowbuf, y_recv, y_send, src, odd, c)
+        copy(rowbuf.at[src, c], rowbuf.at[src, c], y_send.at[2, c], y_recv.at[2, c], y_at(step)).start()
+        src = (z - step + 4) % 4
+        got(colbuf, z_recv, z_send, src, odd, c)
+        copy(colbuf.at[src, c], colbuf.at[src, c], z_send.at[2, c], z_recv.at[2, c], z_at(step)).start()
+
+    def product(c, first):
+        odd = c % 2
+        step = 1 - 2 * odd
+        got(rowbuf, y_recv, y_send, (y + step + 4) % 4, 1 - odd, c)
+        got(colbuf, z_recv, z_send, (z + step + 4) % 4, 1 - odd, c)
+        got(rowbuf, y_recv, y_send, (y + 2) % 4, 2, c)
+        got(colbuf, z_recv, z_send, (z + 2) % 4, 2, c)
+        for k in range(4):
+            high, low = split(colbuf[k, c])
+            colh[k * rows:(k + 1) * rows] = high
+            coll[k * rows:(k + 1) * rows] = low
+
+        def part(k, _):
+            term = dot3(split(rowbuf[k, c]), (colh[...], coll[...]), NT)
+            acc[k] = term if first else acc[k] + term
+            return 0
+
+        lax.fori_loop(0, 4, part, 0)
+
+    @pl.when(jnp.logical_not(same))
+    def _():
+        def send(c, _):
+            copy(own.at[c], colbuf.at[z, c], s_send.at[c], s_recv.at[c], swap).start()
+            return 0
+
+        lax.fori_loop(0, chunks, send, 0)
+
+    y_own(0)
+    y_own(1)
+    rowbuf[y] = own[...]
+
+    @pl.when(same)
+    def _():
+        colbuf[z] = own[...]
+
+    z_own(0)
+    z_own(1)
+    y_own(2)
+    forward(0)
+    z_own(2)
+    y_own(3)
+    forward(1)
+    product(0, True)
+
+    def step(c, _):
+        @pl.when(c + 1 < chunks)
+        def _():
+            z_own(c + 1)
+
+        @pl.when(c + 2 < chunks)
+        def _():
+            y_own(c + 2)
+
+        forward(c)
+        product(c - 1, False)
+        return 0
+
+    lax.fori_loop(2, chunks, step, 0)
+    product(chunks - 1, False)
+
+    mine = pl.ds(pl.multiple_of(core * half, 128), half)
+    theirs = pl.ds(pl.multiple_of((1 - core) * half, 128), half)
+    trade = copy(acc.at[:, :, theirs], exch, t_send.at[3], t_recv.at[3], mate)
+    trade.start()
+    trade.wait()
+
+    total[...] = acc[:, :, mine] + exch[...]
+    sends = []
+    for k, offset in enumerate((2, 1, -1)):
+        to = (y + offset + 4) % 4
+        sends.append(copy(total.at[to], final.at[y], t_send.at[k], t_recv.at[k], y_at(offset)))
+        sends[-1].start()
+    final[y] = total[y]
+    for k, offset in enumerate((2, 1, -1)):
+        src = (y - offset + 4) % 4
+        copy(final.at[src], final.at[src], t_send.at[k], t_recv.at[k], mate).wait_recv()
+    for k in range(2):
+        for q in range(4):
+            place = (k * 4 + q) * rows
+            out[:, place:place + rows] = final[q, :, k * rows:(k + 1) * rows]
+    for one in sends:
+        one.wait_send()
+
+    def drain(c, _):
+        for k in range(3):
+            copy(own.at[c], own.at[c], y_send.at[k, c], y_recv.at[k, c], mate).wait_send()
+            copy(own.at[c], own.at[c], z_send.at[k, c], z_recv.at[k, c], mate).wait_send()
+
+        @pl.when(jnp.logical_not(same))
+        def _():
+            copy(own.at[c], own.at[c], s_send.at[c], s_recv.at[c], swap).wait_send()
+
+        return 0
+
+    lax.fori_loop(0, chunks, drain, 0)
+
+
+def gram(own):
+    chunks, rows, depth = own.shape
+    dma = pltpu.SemaphoreType.DMA
+    return pl.pallas_call(
+        gram_kernel,
+        out_shape=jax.ShapeDtypeStruct((rows, 8 * rows), F32),
+        in_specs=[pl.BlockSpec(memory_space=pltpu.VMEM)],
+        out_specs=pl.BlockSpec(memory_space=pltpu.VMEM),
+        scratch_shapes=[
+            pltpu.VMEM((4, chunks, rows, depth), F32),
+            pltpu.VMEM((4, chunks, rows, depth), F32),
+            pltpu.VMEM((4, rows, 4 * rows), F32),
+            pltpu.VMEM((4 * rows, depth), BF16),
+            pltpu.VMEM((4 * rows, depth), BF16),
+            pltpu.VMEM((4, rows, 2 * rows), F32),
+            pltpu.VMEM((4, rows, 2 * rows), F32),
+            pltpu.VMEM((4, rows, 2 * rows), F32),
+            dma((3, chunks)), dma((3, chunks)), dma((3, chunks)), dma((3, chunks)),
+            dma((chunks,)), dma((chunks,)), dma((4,)), dma((4,)),
+        ],
+        compiler_params=pltpu.CompilerParams(
+            collective_id=1, has_side_effects=True, vmem_limit_bytes=50 * 2**20),
+    )(own)
 
 
 def after_section(solved, own_rows, rhs_rows, diag_inverse, first, reach):
@@ -51,40 +279,27 @@
     sub_count = lax.axis_size("sub")
     round_width = sub_count * piece_len
     pair_cols = local_rhs.shape[3]
-    shaped = factor_rows.reshape(rounds, piece_len, rounds, round_width)
-    round_ids = jnp.arange(rounds)
-    own_diag = shaped[round_ids, :, round_ids, :]
+    own_diag = jnp.stack([factor_rows[k, 0, :, k * round_width:(k + 1) * round_width] for k in range(rounds)])
     diag_blocks = lax.all_gather(own_diag[:, None], "sub", axis=1, tiled=True).reshape(
         rounds, round_width, round_width
     )
-    identity = jnp.broadcast_to(
-        jnp.eye(round_width, dtype=jnp.float32), (rounds, round_width, round_width)
-    )
-    diag_inverse = jax.scipy.linalg.solve_triangular(diag_blocks, identity, lower=True)
+    diag_inverse = diag_inverses(diag_blocks)
     rhs_rows = local_rhs[:, 0]
     own_rows = factor_rows[:, 0]
-    solved_start = jnp.zeros((rounds, round_width, pair_cols), jnp.float32)
+    solved = jnp.zeros((rounds, round_width, pair_cols), jnp.float32)
     section_count = min(8, rounds)
     per_section = rounds // section_count
-    solved = solved_start
     for section_id in range(section_count):
         solved = after_section(
-            solved,
-            own_rows,
-            rhs_rows,
-            diag_inverse,
-            section_id * per_section,
-            (section_id + 1) * per_section,
+            solved, own_rows, rhs_rows, diag_inverse,
+            section_id * per_section, (section_id + 1) * per_section,
         )
     sub_index = lax.axis_index("sub")
     total_pairs = pair_cols * lax.axis_size("blk")
     quarter = total_pairs // sub_count
-    solved_full = solved.reshape(rounds, sub_count, piece_len, pair_cols)
-    own_part = lax.dynamic_index_in_dim(solved_full, sub_index, 1, keepdims=False).reshape(
-        rounds * piece_len, pair_cols
-    )
-    product = transposed_dot(own_part, lax.all_gather(own_part, "blk", axis=1, tiled=True))
-    coulomb = lax.psum_scatter(product, "sub", scatter_dimension=1, tiled=True)
+    core_half = lax.dynamic_slice_in_dim(solved, (sub_index % 2) * (rounds // 2), rounds // 2)
+    own = core_half.reshape(8, rounds // 2 * round_width // 8, pair_cols).transpose(0, 2, 1)
+    coulomb = gram(own)
     slab_start = slab_index[0] * NOCC
     occ_slab = lax.dynamic_slice_in_dim(occ_energy, slab_start, NOCC)
     pair_energy = jnp.repeat(occ_slab, NVIRT) - jnp.tile(virt_energy, NOCC)

time: 1060 us -> 564 us (0.53)
  other arithmetic: 354 us -> 34.1 us
  waiting for transfers between devices: 263 us -> 9.53 us
  Pallas kernels: 0 us -> 156 us
  matrix products: 149 us -> 100 us
  local copies, waits for them, and re-layouts: 79.6 us -> 51 us
    another operation x4 -> x1, other arithmetic: 319 us -> 0.95 us  [the longest x3 317 us: shards(): jax.scipy.linalg.solve_triangular(diag_blocks, identity, lower=True)]
    all_gather x1 -> x0, waiting for transfers between devices: 204 us -> none  [shards(): lax.all_gather(own_part, 'blk', axis=1, tiled=True)]
    pallas_call x0 -> x2, Pallas kernels: none -> 156 us  [the longest x1 85.9 us: gram(): pl.pallas_call(gram_kernel, out_shape=jax.ShapeDtypeStruct((rows, 8 * row...]
    reduce_scatter x1 -> x0, waiting for transfers between devices: 49 us -> none  [shards(): coulomb = lax.psum_scatter(product, 'sub', scatter_dimension=1, tiled=True)]
    dot_general x1 -> x0, matrix products: 45.4 us -> none  [transposed_dot(): lax.dot_general(left, right, (((0,), (0,)), ((), ())), precision=PRECISE)]
    reshape x2, local copies, waits for them, and re-layouts: 15 us -> 3.52 us  [shards(): core_half.reshape(8, rounds // 2 * round_width // 8, pair_cols)]
    unnamed x98 -> x78, local copies, waits for them, and re-layouts: 49.4 us -> 40.6 us
  transfers between devices with their start and end apart: 4 -> 2, of which waited for: 3 -> 1; matrix products, arithmetic and copies ran while one was open for 8% -> 11% of each run, Pallas kernels for 0% -> 0%
where the time goes in v1:
time: 564 us; the launch traced here: 554 us
  blocking collectives  177 us (31%)
  Pallas kernels  156 us (28%)
  matrix products  100 us (18%)
  local copies, waits for them, and re-layouts  51 us (9%)
  other arithmetic  34.1 us (6%)
  between operations  15.2 us (3%)
  starting transfers between devices  11.1 us (2%)
  waiting for transfers between devices  9.53 us (2%)
    all_gather x32, blocking collectives, advance(): lax.all_gather(updated[None], 'sub', axis=0, tiled=True)  177 us
    pallas_call x1, Pallas kernels, gram(): pl.pallas_call(gram_kernel, out_shape=jax.ShapeDtypeStruct((rows, 8 * row...  85.9 us
    dot_general x31, matrix products, advance(): jnp.dot(factor_part, solved[:reach].reshape(width, pair_cols), precision=...  82.4 us
    pallas_call x1, Pallas kernels, diag_inverses(): pl.pallas_call(inverse_kernel, grid=(rounds // batch,), in_specs=[spec],...  70.5 us
    unnamed x78, local copies, waits for them, and re-layouts  40.6 us
    unnamed x1, other arithmetic  29.3 us
    dot_general x32, matrix products, advance(): solved_round = jnp.dot(inverse, round_block, precision=PRECISE)  12.8 us
  transfers between devices with their start and end apart: 2, of which 1 were waited for; matrix products, arithmetic and copies ran while one was open for 11% of the time, Pallas kernels for 0%

profile of v1, /device:TPU:5, one launch (start us, length us, event | category | flops | bytes accessed | tf_op | source)
XLA Modules:
  0.0 554.3 jit_solution(6156175114104521758)
XLA Ops:
  35.9 29.3 %reduce.8 = f32[6144,32]{1,0:T(8,128)} reduce(f32[6144,1,1,32]{3,2,1,0:T(1,128)} %bitcast.933, f32[]{:T(128)} %broadcast.55), dimensions={1,2}, to_apply=%bitcast.831.reduce_sub_computation | reduce | bytes 1572868
  69.0 11.1 %all-to-all-start = ((f32[32,1,6144]{2,1,0:T(1,128)}), f32[32,1,6144]{2,1,0:T(1,128)S(1)}, u32[]{:S(2)}, u32[]{:S(2)}) async-start(f32[32,1,6144]{2,1,0:T(1,128)} %reshape.551), calls=%async_computation | async-start | bytes 1572864 | tf_op jit(solution)/shard_map/all_to_all | solution.py:276
  82.7 9.5 %all-to-all-done = f32[32,1,6144]{2,1,0:T(1,128)S(1)} async-done(((f32[32,1,6144]{2,1,0:T(1,128)}), f32[32,1,6144]{2,1,0:T(1,128)S(1)}, u32[]{:S(2)}, u32[]{:S(2)}) %all-to-all-start) | async-done | bytes 786464 | tf_op jit(solution)/shard_map/all_to_all | solution.py:276
  94.6 6.9 %reshape.552 = f32[6144,1,1,32]{3,2,1,0:T(1,128)} reshape(f32[32,6144]{1,0:T(8,128)S(1)} %reduce.9) | data formatting | bytes 1572864
  111.8 7.6 %all_gather.100 = f32[4,32,192]{2,1,0:T(8,128)S(1)} all-gather(f32[1,32,192]{2,1,0:T(8,128)S(1)} %copy.77), channel_id=1, replica_groups=mesh['blk'=32,'sub'=4] {'sub'}, dimensions={0}, use_global_device_ids=true | all-gather | bytes 122880 | tf_op jit(solution)/shard_map/eval_jaxpr/all_gather | solution.py:264
  119.4 70.5 %shard_map.67 = f32[32,128,128]{2,1,0:T(8,128)} custom-call(f32[32,128,128]{2,1,0:T(8,128)} %all-gather.34.cloned.1.call-done.diag_ref), custom_call_target="tpu_custom_call" | custom-call | tf_op jit(solution)/shard_map/pallas_call | solution.py:64
  192.5 5.4 all-gather.1
  207.1 5.4 all-gather.3
  214.6 5.4 all-gather.4
  229.6 5.6 %all-gather.6 = f32[128,192]{1,0:T(8,128)S(1)} all-gather(f32[32,192]{1,0:T(8,128)S(1)} %fusion.224), channel_id=8, replica_groups=mesh['blk'=32,'sub'=4] {'sub'}, dimensions={0}, use_global_device_ids=true | all-gather | bytes 122880 | tf_op jit(solution)/shard_map/eval_jaxpr/all_gather | solution.py:264
  245.2 5.4 all-gather.8
  277.0 5.4 all-gather.12
  293.5 5.8 %all-gather.14 = f32[128,192]{1,0:T(8,128)S(1)} all-gather(f32[32,192]{1,0:T(8,128)S(1)} %fusion.166), channel_id=16, replica_groups=mesh['blk'=32,'sub'=4] {'sub'}, dimensions={0}, use_global_device_ids=true | all-gather | bytes 122880 | tf_op jit(solution)/shard_map/eval_jaxpr/all_gather | solution.py:264
  310.8 5.4 all-gather.16
  336.6 5.4 all-gather.19
  345.6 5.6 %all-gather.20 = f32[128,192]{1,0:T(8,128)S(1)} all-gather(f32[32,192]{1,0:T(8,128)S(1)} %fusion.178), channel_id=22, replica_groups=mesh['blk'=32,'sub'=4] {'sub'}, dimensions={0}, use_global_device_ids=true | all-gather | bytes 122880 | tf_op jit(solution)/shard_map/eval_jaxpr/all_gather | solution.py:264
  354.8 5.4 all-gather.21
  391.4 5.6 %all-gather.25 = f32[128,192]{1,0:T(8,128)S(1)} all-gather(f32[32,192]{1,0:T(8,128)S(1)} %fusion.208), channel_id=27, replica_groups=mesh['blk'=32,'sub'=4] {'sub'}, dimensions={0}, use_global_device_ids=true | all-gather | bytes 122880 | tf_op jit(solution)/shard_map/eval_jaxpr/all_gather | solution.py:264
  401.0 5.4 all-gather.26
  420.1 5.4 all-gather.28
  429.8 5.7 %all-gather.29 = f32[128,192]{1,0:T(8,128)S(1)} all-gather(f32[32,192]{1,0:T(8,128)S(1)} %fusion.136), channel_id=31, replica_groups=mesh['blk'=32,'sub'=4] {'sub'}, dimensions={0}, use_global_device_ids=true | all-gather | bytes 122880 | tf_op jit(solution)/shard_map/eval_jaxpr/all_gather | solution.py:264
  439.8 5.4 all-gather.30
  449.5 5.4 all-gather.31
  459.8 85.9 %shard_map.68 = f32[192,1536]{1,0:T(8,128)S(1)} custom-call(f32[8,192,256]{2,1,0:T(8,128)S(1)} %bitcast.932), custom_call_target="tpu_custom_call" | custom-call | tf_op jit(solution)/shard_map/pallas_call | solution.py:230
  (176 shorter events, 224.9 us)
Async XLA Ops:
  6.5 24.0 %copy-start = (f32[1,1,32,6144]{3,2,1,0:T(8,128)S(1)}, f32[1,1,32,6144]{3,2,1,0:T(8,128)}, u32[]{:S(2)}) copy-start(f32[1,1,32,6144]{3,2,1,0:T(8,128)} %param.6) | copy-start | bytes 2359300
  6.5 112.9 %all-gather.34.cloned.1.call-start = ((), (), s32[]{:S(2)}) async-start(), calls=%async_computation.1 | async-start | bytes 2621440 | tf_op jit(solution)/shard_map/all_gather | solution.py:283
  29.6 0.8 copy-start.2
  65.3 16.2 %copy-start.5 = (f32[2048]{0:T(1024)S(1)}, f32[2048]{0:T(1024)}, u32[]{:S(2)}) copy-start(f32[2048]{0:T(1024)} %param.11) | copy-start | bytes 24580
  69.0 23.3 %all-to-all-start = ((f32[32,1,6144]{2,1,0:T(1,128)}), f32[32,1,6144]{2,1,0:T(1,128)S(1)}, u32[]{:S(2)}, u32[]{:S(2)}) async-start(f32[32,1,6144]{2,1,0:T(1,128)} %reshape.551), calls=%async_computation | async-start | bytes 1572864 | tf_op jit(solution)/shard_map/all_to_all | solution.py:276
  190.0 8.3 %copy-start.1 = (f32[32,128,128]{2,1,0:T(8,128)S(1)}, f32[32,128,128]{2,1,0:T(8,128)}, u32[]{:S(2)}) copy-start(f32[32,128,128]{2,1,0:T(8,128)} %shard_map.67) | copy-start | bytes 6291460
  420.0 15.8 %copy-start.4 = (f32[1,1,32,1,192]{4,2,3,1,0:T(8,128)S(1)}, f32[1,1,32,1,192]{4,2,3,1,0:T(8,128)}, u32[]{:S(2)}) copy-start(f32[1,1,32,1,192]{4,2,3,1,0:T(8,128)} %copy.204) | copy-start | bytes 73732
  429.8 15.8 %copy-start.3 = (f32[1,1,32,1,192]{4,2,3,1,0:T(8,128)S(1)}, f32[1,1,32,1,192]{4,2,3,1,0:T(8,128)}, u32[]{:S(2)}) copy-start(f32[1,1,32,1,192]{4,2,3,1,0:T(8,128)} %copy.205) | copy-start | bytes 73732
Sparse Core Ops, SparseCore 0:
  30.6 31.5 all-gather.33

commit v2 on v1

--- a/solution.py
+++ b/solution.py
@@ -29,50 +29,222 @@
     return one(a[0], b[0]) + (one(a[0], b[1]) + one(a[1], b[0]))
 
 
-def canonical_order(integrals, slot_order):
-    piece_len = integrals.shape[2]
-    places = jnp.arange(piece_len, dtype=jnp.int32)
-    onehot = (slot_order[..., None] == places).astype(jnp.float32)
-    return jnp.einsum("rscq,rscp->rsqp", onehot, integrals, precision=PRECISE)
-
-
-def inverse_of(block):
-    n = block.shape[0]
-    row = lax.broadcasted_iota(jnp.int32, (n, n), 0)
-    col = lax.broadcasted_iota(jnp.int32, (n, n), 1)
-    diag = jnp.sum(jnp.where(row == col, block, 0.0), axis=1, keepdims=True)
-    inv = jnp.where(row == col, 1.0 / diag, 0.0)
-    size = 1
-    while size < n:
-        below = (row // size == col // size + 1) & (row // (2 * size) == col // (2 * size))
-        part = split(jnp.where(below, block, 0.0))
-        now = split(inv)
-        inv = inv - dot3(now, split(dot3(part, now, NN)), NN)
-        size *= 2
-    return inv
-
-
-def inverse_kernel(diag_ref, inv_ref):
-    for k in range(diag_ref.shape[0]):
-        inv_ref[k] = inverse_of(diag_ref[k])
-
-
-def diag_inverses(diag_blocks):
-    rounds, width, _ = diag_blocks.shape
-    batch = 8
-    spec = pl.BlockSpec((batch, width, width), lambda i: (i, 0, 0))
+def copy(src, dst, send, recv, who):
+    return pltpu.make_async_remote_copy(
+        src_ref=src, dst_ref=dst, send_sem=send, recv_sem=recv,
+        device_id=who, device_id_type=MESH)
+
+
+def panel_place(i, r):
+    if isinstance(i, int):
+        return (i, r - 2 * i) if i < 8 else (15 - i, r + 2)
+    return jnp.where(i < 8, i, 15 - i), jnp.where(i < 8, r - 2 * i, r + 2)
+
+
+def solve_kernel(integrals, slots, factor, out, pan, blocks, half_inv, half_tmp, dinv, sb, rhs, gbuf,
+                 xh, xlow, xbuf, tx, xt,
+                 pan_local, pan_send, pan_recv, diag_send, diag_recv, a_send, a_recv,
+                 inv_send, inv_recv, g_send, g_recv, x_send, x_recv):
+    blk, sub = lax.axis_index("blk"), lax.axis_index("sub")
+    hi = blk // 16
+    xl, core = sub // 2, sub % 2
+    x = 2 * hi + xl
+    mate = {"blk": blk, "sub": sub + 1 - 2 * core}
+    peer = {"blk": blk, "sub": sub + 2 - 4 * xl}
+
+    def beside(offset, to_core):
+        other = (x + offset + 4) % 4
+        return {"blk": blk + (other // 2 - hi) * 16, "sub": (other % 2) * 2 + to_core}
+
+    for i in range(16):
+        for q in range(2):
+            copy(factor.at[2 * i + q, :, 256 * i:256 * i + 256], blocks.at[i // 2, q, xl, core],
+                 diag_send, diag_recv, beside(1 if i < 8 else -1, i % 2)).start()
+    for i in range(16):
+        k, row = panel_place(i, 2 * i)
+        piece = factor.at[2 * i:32, :, 256 * i:256 * i + 256]
+        place = pan.at[k, row:row + 32 - 2 * i, core]
+        pltpu.make_async_copy(piece, place, pan_local.at[i]).start()
+        copy(piece, place, pan_send.at[i], pan_recv.at[i], mate).start()
+
+    onehot = (slots[...] == lax.broadcasted_iota(jnp.int32, (32, 32), 0)).astype(F32).astype(BF16)
+
+    def pick(v):
+        return lax.dot_general(onehot, v, NN, preferred_element_type=F32)
+
+    for g in range(16):
+        value = integrals[:, 384 * g:384 * g + 384]
+        high = value.astype(BF16)
+        rest = value - high.astype(F32)
+        mid = rest.astype(BF16)
+        low = (rest - mid.astype(F32)).astype(BF16)
+        picked = pick(high) + (pick(mid) + pick(low))
+        for k in range(4):
+            sb[4 * g + k] = picked[:, 96 * k:96 * k + 96]
+
+    def spread(k, _):
+        to = (blk + k) % 32
+        for c in range(2):
+            copy(sb.at[2 * to + c], rhs.at[2 * blk + core], a_send, a_recv,
+                 {"blk": to, "sub": 2 * xl + c}).start()
+        return 0
+
+    lax.fori_loop(1, 32, spread, 0)
+    copy(sb.at[2 * blk + 1 - core], rhs.at[2 * blk + core], a_send, a_recv, mate).start()
+    rhs[2 * blk + core] = sb[2 * blk + core]
+
+    for i in range(16):
+        k, row = panel_place(i, 2 * i)
+        piece = pan.at[k, row:row + 32 - 2 * i, core]
+        pltpu.make_async_copy(piece, piece, pan_local.at[i]).wait()
+        copy(piece, piece, pan_send.at[i], pan_recv.at[i], mate).wait_recv()
+    copy(blocks.at[0:4], blocks.at[0:4], diag_send, diag_recv, mate).wait_recv()
+
+    def place_own(j, _):
+        k, row = panel_place(2 * j + core, 2 * (2 * j + core))
+        for q in range(2):
+            blocks[j, q, xl] = pan[k, row + q]
+        return 0
+
+    lax.fori_loop(0, 8, place_own, 0)
+
+    row = lax.broadcasted_iota(jnp.int32, (128, 128), 0)
+    col = lax.broadcasted_iota(jnp.int32, (128, 128), 1)
+
+    def invert(g, _):
+        def block(n):
+            q = n % 2
+            return blocks[2 * g + n // 2, q, :, :, :, 128 * q:128 * q + 128].reshape(128, 128)
+
+        for n in range(4):
+            value = block(n)
+            diag = jnp.where(row == col, value, 0.0)
+            down = 1.0 / jnp.sum(diag, axis=1, keepdims=True)
+            across = 1.0 / jnp.sum(diag, axis=0, keepdims=True)
+            below = (row == col + 1) & (row % 2 == 1)
+            half_inv[4 * g + n] = jnp.where(row == col, down, 0.0) - jnp.where(below, value * down * across, 0.0)
+        size = 2
+        while size < 128:
+            below = (row // size == col // size + 1) & (row // (2 * size) == col // (2 * size))
+            for n in range(4):
+                part = jnp.where(below, block(n), 0.0)
+                half_tmp[n] = dot3(split(part), split(half_inv[4 * g + n]), NN)
+            for n in range(4):
+                now = half_inv[4 * g + n]
+                half_inv[4 * g + n] = now - dot3(split(now), split(half_tmp[n]), NN)
+            size *= 2
+        for n in range(2):
+            lower = blocks[2 * g + n, 1, :, :, :, 0:128].reshape(128, 128)
+            half_tmp[n] = dot3(split(lower), split(half_inv[4 * g + 2 * n]), NN)
+        for n in range(2):
+            i = 2 * (2 * g + n) + core
+            dinv[i, 0:128, 0:128] = half_inv[4 * g + 2 * n]
+            dinv[i, 128:256, 128:256] = half_inv[4 * g + 2 * n + 1]
+            dinv[i, 0:128, 128:256] = jnp.zeros((128, 128), F32)
+            dinv[i, 128:256, 0:128] = -dot3(split(half_inv[4 * g + 2 * n + 1]), split(half_tmp[n]), NN)
+        return 0
+
+    lax.fori_loop(0, 4, invert, 0)
+
+    def share(j, _):
+        copy(dinv.at[2 * j + core], dinv.at[2 * j + core], inv_send, inv_recv, mate).start()
+        return 0
+
+    lax.fori_loop(0, 8, share, 0)
+    copy(rhs.at[0:63], rhs.at[0:63], a_send, a_recv, mate).wait_recv()
+    copy(dinv.at[0:8], dinv.at[0:8], inv_send, inv_recv, mate).wait_recv()
+
+    def offer(i, value):
+        gbuf[i, :, xl] = value.reshape(2, 64, 96)
+        copy(gbuf.at[i, :, xl], gbuf.at[i, :, xl], g_send.at[i], g_recv.at[i], peer).start()
+
+    def factor_part(i, t):
+        k, at = panel_place(i, 2 * t)
+        return split(pan[k, pl.ds(at, 2)].reshape(128, 256))
+
+    offer(0, rhs[0:4].reshape(128, 96))
+
+    def round_of(i, _):
+        inverse = split(dinv[i])
+
+        @pl.when(i > 0)
+        def _():
+            def later(t, _):
+                term = dot3(factor_part(i - 1, t), (xh[...], xlow[...]), NN)
+                rows = pl.ds(4 * t, 4)
+                rhs[rows] = rhs[rows] - term.reshape(4, 32, 96)
+                return 0
+
+            lax.fori_loop(i + 1, 16, later, 0)
+
+        other = gbuf.at[i, :, 1 - xl]
+        copy(other, other, g_send.at[i], g_recv.at[i], peer).wait_recv()
+        solved = dot3(inverse, split(gbuf[i].reshape(256, 96)), NN)
+        high, low = split(solved)
+        xh[...] = high
+        xlow[...] = low
+
+        @pl.when(i < 15)
+        def _():
+            term = dot3(factor_part(i, i + 1), (high, low), NN)
+            offer(i + 1, rhs[pl.ds(4 * i + 4, 4)].reshape(128, 96) - term)
+
+        xbuf[...] = solved.reshape(2, 128, 96)
+        tx[i] = xbuf[1 - core].T
+        copy(tx.at[i], xt.at[i, core], x_send, x_recv, mate).start()
+        xt[i, core] = xbuf[core].T
+        return 0
+
+    lax.fori_loop(0, 16, round_of, 0)
+
+    copy(tx, tx, x_send, x_recv, mate).wait_recv()
+    out[...] = xt[...]
+
+    for i in range(16):
+        k, row = panel_place(i, 2 * i)
+        piece = pan.at[k, row:row + 32 - 2 * i, core]
+        copy(piece, piece, pan_send.at[i], pan_recv.at[i], mate).wait_send()
+        mine = gbuf.at[i, :, xl]
+        copy(mine, mine, g_send.at[i], g_recv.at[i], peer).wait_send()
+    copy(blocks.at[0:4], blocks.at[0:4], diag_send, diag_recv, mate).wait_send()
+    copy(sb.at[0:63], sb.at[0:63], a_send, a_recv, mate).wait_send()
+    copy(dinv.at[0:8], dinv.at[0:8], inv_send, inv_recv, mate).wait_send()
+    copy(tx, tx, x_send, x_recv, mate).wait_send()
+
+
+def solve(integrals, slots, factor):
+    dma = pltpu.SemaphoreType.DMA
+    vmem = pl.BlockSpec(memory_space=pltpu.VMEM)
     return pl.pallas_call(
-        inverse_kernel,
-        grid=(rounds // batch,),
-        in_specs=[spec],
-        out_specs=spec,
-        out_shape=jax.ShapeDtypeStruct(diag_blocks.shape, F32),
-    )(diag_blocks)
+        solve_kernel,
+        out_shape=jax.ShapeDtypeStruct((16, 2, 96, 128), F32),
+        in_specs=[vmem, vmem, pl.BlockSpec(memory_space=pl.ANY)],
+        out_specs=vmem,
+        scratch_shapes=[
+            pltpu.VMEM((8, 34, 2, 32, 256), F32),
+            pltpu.VMEM((8, 2, 2, 2, 32, 256), F32),
+            pltpu.VMEM((16, 128, 128), F32),
+            pltpu.VMEM((4, 128, 128), F32),
+            pltpu.VMEM((16, 256, 256), F32),
+            pltpu.VMEM((64, 32, 96), F32),
+            pltpu.VMEM((64, 32, 96), F32),
+            pltpu.VMEM((16, 2, 2, 64, 96), F32),
+            pltpu.VMEM((256, 96), BF16),
+            pltpu.VMEM((256, 96), BF16),
+            pltpu.VMEM((2, 128, 96), F32),
+            pltpu.VMEM((16, 96, 128), F32),
+            pltpu.VMEM((16, 2, 96, 128), F32),
+            dma((16,)), dma((16,)), dma((16,)), dma, dma, dma, dma, dma, dma,
+            dma((16,)), dma((16,)), dma, dma,
+        ],
+        compiler_params=pltpu.CompilerParams(
+            has_side_effects=True, vmem_limit_bytes=56 * 2**20),
+    )(integrals, slots, factor)
 
 
 def gram_kernel(own, out, rowbuf, colbuf, acc, colh, coll, exch, total, final,
                 y_send, y_recv, z_send, z_recv, s_send, s_recv, t_send, t_recv):
-    chunks, rows, depth = own.shape
+    chunks, _, rows, depth = own.shape
     half = 2 * rows
     blk, sub = lax.axis_index("blk"), lax.axis_index("sub")
     y, z, xh = blk % 4, (blk // 4) % 4, blk // 16
@@ -93,10 +265,8 @@
         pl.semaphore_signal(barrier, inc=1, device_id=who, device_id_type=MESH)
     pl.semaphore_wait(barrier, 7)
 
-    def copy(src, dst, send, recv, who):
-        return pltpu.make_async_remote_copy(
-            src_ref=src, dst_ref=dst, send_sem=send, recv_sem=recv,
-            device_id=who, device_id_type=MESH)
+    def whole(buf, k, c):
+        return jnp.concatenate([buf[k, c, 0], buf[k, c, 1]], axis=1)
 
     def y_own(c):
         for k, offset in enumerate((1, -1)):
@@ -135,12 +305,12 @@
         got(rowbuf, y_recv, y_send, (y + 2) % 4, 2, c)
         got(colbuf, z_recv, z_send, (z + 2) % 4, 2, c)
         for k in range(4):
-            high, low = split(colbuf[k, c])
+            high, low = split(whole(colbuf, k, c))
             colh[k * rows:(k + 1) * rows] = high
             coll[k * rows:(k + 1) * rows] = low
 
         def part(k, _):
-            term = dot3(split(rowbuf[k, c]), (colh[...], coll[...]), NT)
+            term = dot3(split(whole(rowbuf, k, c)), (colh[...], coll[...]), NT)
             acc[k] = term if first else acc[k] + term
             return 0
 
@@ -225,7 +395,7 @@
 
 
 def gram(own):
-    chunks, rows, depth = own.shape
+    chunks, _, rows, depth = own.shape
     dma = pltpu.SemaphoreType.DMA
     return pl.pallas_call(
         gram_kernel,
@@ -233,11 +403,11 @@
         in_specs=[pl.BlockSpec(memory_space=pltpu.VMEM)],
         out_specs=pl.BlockSpec(memory_space=pltpu.VMEM),
         scratch_shapes=[
-            pltpu.VMEM((4, chunks, rows, depth), F32),
-            pltpu.VMEM((4, chunks, rows, depth), F32),
+            pltpu.VMEM((4, chunks, 2, rows, depth), F32),
+            pltpu.VMEM((4, chunks, 2, rows, depth), F32),
             pltpu.VMEM((4, rows, 4 * rows), F32),
-            pltpu.VMEM((4 * rows, depth), BF16),
-            pltpu.VMEM((4 * rows, depth), BF16),
+            pltpu.VMEM((4 * rows, 2 * depth), BF16),
+            pltpu.VMEM((4 * rows, 2 * depth), BF16),
             pltpu.VMEM((4, rows, 2 * rows), F32),
             pltpu.VMEM((4, rows, 2 * rows), F32),
             pltpu.VMEM((4, rows, 2 * rows), F32),
@@ -249,62 +419,15 @@
     )(own)
 
 
-def after_section(solved, own_rows, rhs_rows, diag_inverse, first, reach):
-    round_width = diag_inverse.shape[1]
-    pair_cols = solved.shape[2]
-    width = reach * round_width
-    rows_part = own_rows[:, :, :width]
-
-    def advance(round_id, solved):
-        factor_part = lax.dynamic_index_in_dim(rows_part, round_id, 0, keepdims=False)
-        known_part = jnp.dot(
-            factor_part, solved[:reach].reshape(width, pair_cols), precision=PRECISE
-        )
-        updated = lax.dynamic_index_in_dim(rhs_rows, round_id, 0, keepdims=False) - known_part
-        round_block = lax.all_gather(updated[None], "sub", axis=0, tiled=True).reshape(
-            round_width, pair_cols
-        )
-        inverse = lax.dynamic_index_in_dim(diag_inverse, round_id, 0, keepdims=False)
-        solved_round = jnp.dot(inverse, round_block, precision=PRECISE)
-        return lax.dynamic_update_index_in_dim(solved, solved_round, round_id, 0)
-
-    return lax.fori_loop(first, reach, advance, solved, unroll=True)
-
-
 def shards(integrals, slot_order, factor_rows, occ_energy, slab_index, virt_energy):
-    canonical = canonical_order(integrals, slot_order)
-    local_rhs = lax.all_to_all(canonical, "blk", split_axis=3, concat_axis=0, tiled=True)
-    rounds = factor_rows.shape[0]
-    piece_len = factor_rows.shape[2]
-    sub_count = lax.axis_size("sub")
-    round_width = sub_count * piece_len
-    pair_cols = local_rhs.shape[3]
-    own_diag = jnp.stack([factor_rows[k, 0, :, k * round_width:(k + 1) * round_width] for k in range(rounds)])
-    diag_blocks = lax.all_gather(own_diag[:, None], "sub", axis=1, tiled=True).reshape(
-        rounds, round_width, round_width
-    )
-    diag_inverse = diag_inverses(diag_blocks)
-    rhs_rows = local_rhs[:, 0]
-    own_rows = factor_rows[:, 0]
-    solved = jnp.zeros((rounds, round_width, pair_cols), jnp.float32)
-    section_count = min(8, rounds)
-    per_section = rounds // section_count
-    for section_id in range(section_count):
-        solved = after_section(
-            solved, own_rows, rhs_rows, diag_inverse,
-            section_id * per_section, (section_id + 1) * per_section,
-        )
-    sub_index = lax.axis_index("sub")
-    total_pairs = pair_cols * lax.axis_size("blk")
-    quarter = total_pairs // sub_count
-    core_half = lax.dynamic_slice_in_dim(solved, (sub_index % 2) * (rounds // 2), rounds // 2)
-    own = core_half.reshape(8, rounds // 2 * round_width // 8, pair_cols).transpose(0, 2, 1)
-    coulomb = gram(own)
+    fitted = solve(integrals[0, 0], slot_order[0], factor_rows[:, 0])
+    coulomb = gram(fitted.reshape(8, 2, 192, 128))
+    pair_rows, quarter = coulomb.shape
     slab_start = slab_index[0] * NOCC
     occ_slab = lax.dynamic_slice_in_dim(occ_energy, slab_start, NOCC)
     pair_energy = jnp.repeat(occ_slab, NVIRT) - jnp.tile(virt_energy, NOCC)
-    row_energy = lax.dynamic_slice_in_dim(pair_energy, lax.axis_index("blk") * pair_cols, pair_cols)
-    col_energy = lax.dynamic_slice_in_dim(pair_energy, sub_index * quarter, quarter)
+    row_energy = lax.dynamic_slice_in_dim(pair_energy, lax.axis_index("blk") * pair_rows, pair_rows)
+    col_energy = lax.dynamic_slice_in_dim(pair_energy, lax.axis_index("sub") * quarter, quarter)
     return coulomb / (row_energy[:, None] + col_energy[None, :])
 
 

time: 564 us -> 202 us (0.36); the launches traced: 554 us -> 200 us
  blocking collectives: 177 us -> 0 us
  matrix products: 100 us -> 0 us
  local copies, waits for them, and re-layouts: 51 us -> 2.34 us
  Pallas kernels: 156 us -> 196 us
  other arithmetic: 34.1 us -> 1.32 us
  between operations: 15.2 us -> 0.69 us
  starting transfers between devices: 11.1 us -> 0 us
  waiting for transfers between devices: 9.53 us -> 0 us
    all_gather x32 -> x0, blocking collectives: 177 us -> none  [advance(): lax.all_gather(updated[None], 'sub', axis=0, tiled=True)]
    dot_general x64 -> x0, matrix products: 100 us -> none  [the longest x31 82.4 us: advance(): jnp.dot(factor_part, solved[:reach].reshape(width, pair_cols), precision=...]
    pallas_call x1, Pallas kernels: 70.5 us -> 114 us  [solve(): pl.pallas_call(solve_kernel, out_shape=jax.ShapeDtypeStruct((16, 2, 96, 1...]
    unnamed x78 -> x4, local copies, waits for them, and re-layouts: 40.6 us -> 1.4 us
    unnamed x1 -> x0, other arithmetic: 29.3 us -> none
    all_to_all x1 -> x0, starting transfers between devices: 11.1 us -> none  [shards(): lax.all_to_all(canonical, 'blk', split_axis=3, concat_axis=0, tiled=True)]
    all_to_all x1 -> x0, waiting for transfers between devices: 9.52 us -> none  [shards(): lax.all_to_all(canonical, 'blk', split_axis=3, concat_axis=0, tiled=True)]
  transfers between devices with their start and end apart: 2 -> 0, of which waited for: 1 -> 0; matrix products, arithmetic and copies ran while one was open for 11% -> 0% of each run, Pallas kernels for 0% -> 0%
where the time goes in v2:
time: 202 us; the launch traced here: 200 us
  Pallas kernels  196 us (97%)
  local copies, waits for them, and re-layouts  2.34 us (1%)
    pallas_call x1, Pallas kernels, solve(): pl.pallas_call(solve_kernel, out_shape=jax.ShapeDtypeStruct((16, 2, 96, 1...  114 us
    pallas_call x1, Pallas kernels, gram(): pl.pallas_call(gram_kernel, out_shape=jax.ShapeDtypeStruct((rows, 8 * row...  81.8 us

profile of v2, /device:TPU:5, one launch (start us, length us, event | category | flops | bytes accessed | tf_op | source)
XLA Modules:
  0.0 199.9 jit_solution(10317723203054567561)
XLA Ops:
  0.0 113.7 %shard_map.64 = f32[16,2,96,128]{3,2,1,0:T(8,128)} custom-call(f32[32,6144]{1,0:T(8,128)} %bitcast.7, s32[1,32]{1,0:T(1,128)} %bitcast.8, f32[32,32,4096]{2,1,0:T(8,128)} %bitcast.6), custom_call_target="tpu_custom_call" | custom-call | tf_op jit(solution)/shard_map/pallas_call | solution.py:218
  113.7 0.0 copy-start
  113.7 1.4 copy-done
  115.1 0.0 copy-start.1
  115.1 81.8 %shard_map.65 = f32[192,1536]{1,0:T(8,128)S(1)} custom-call(f32[8,2,192,128]{3,2,1,0:T(8,128)S(1)} %bitcast.5), custom_call_target="tpu_custom_call" | custom-call | tf_op jit(solution)/shard_map/pallas_call | solution.py:400
  197.6 0.8 dynamic_slice.9
  198.4 0.0 copy-done.1
  198.4 0.1 broadcast_subtract_fusion
  198.5 0.1 dynamic_slice.11
  198.5 0.1 dynamic_slice.10
  198.6 1.2 add_divide_fusion
  (1 shorter events, 0.0 us)
Async XLA Ops:
  113.7 1.4 copy-start
  115.1 83.2 %copy-start.1 = (f32[2048]{0:T(1024)S(1)}, f32[2048]{0:T(1024)}, u32[]{:S(2)}) copy-start(f32[2048]{0:T(1024)} %param.11) | copy-start | bytes 24580

commit v3 on v2

v3 whole, which is shorter than its diff:
```python
import functools

import jax
import jax.numpy as jnp
from jax import lax
from jax.experimental import pallas as pl
from jax.experimental.pallas import tpu as pltpu
from jax.sharding import PartitionSpec as P

NVIRT = 2048
NOCC = 3
PRECISE = lax.Precision.HIGHEST
F32 = jnp.float32
BF16 = jnp.bfloat16
MESH = pl.DeviceIdType.MESH
NN = (((1,), (0,)), ((), ()))
NT = (((1,), (1,)), ((), ()))


def split(x):
    high = x.astype(BF16)
    return high, (x - high.astype(F32)).astype(BF16)


def dot3(a, b, dims):
    def one(p, q):
        return lax.dot_general(p, q, dims, preferred_element_type=F32)

    return one(a[0], b[0]) + (one(a[0], b[1]) + one(a[1], b[0]))


def copy(src, dst, send, recv, who):
    return pltpu.make_async_remote_copy(
        src_ref=src, dst_ref=dst, send_sem=send, recv_sem=recv,
        device_id=who, device_id_type=MESH)


def panel_place(i, r):
    if isinstance(i, int):
        return (i, r - 2 * i) if i < 8 else (15 - i, r + 2)
    return jnp.where(i < 8, i, 15 - i), jnp.where(i < 8, r - 2 * i, r + 2)


def fused_kernel(integrals, slots, factor, out, pan, blocks, half_inv, half_tmp, dinv, sb, rhs, gbuf,
                 xh, xlow, xbuf, tx, rowbuf, colbuf, acc, colh, coll, exch, total, final, relay,
                 pan_local, pan_send, pan_recv, diag_send, diag_recv, a_send, a_recv,
                 inv_send, inv_recv, g_send, g_recv, x_send, x_recv,
                 y_send, y_recv, z_send, z_recv, s_send, s_recv, t_send, t_recv, e_send, e_recv):
    blk, sub = lax.axis_index("blk"), lax.axis_index("sub")
    hi = blk // 16
    xl, core = sub // 2, sub % 2
    x = 2 * hi + xl
    y, z = blk % 4, (blk // 4) % 4
    same = hi == xl
    mate = {"blk": blk, "sub": sub + 1 - 2 * core}
    peer = {"blk": blk, "sub": sub + 2 - 4 * xl}

    def beside(offset, to_core):
        other = (x + offset + 4) % 4
        return {"blk": blk + (other // 2 - hi) * 16, "sub": (other % 2) * 2 + to_core}

    def y_at(offset):
        return {"blk": blk - y + (y + offset + 4) % 4, "sub": sub}

    def z_at(offset):
        return {"blk": blk - 4 * z + 4 * ((z + offset + 4) % 4), "sub": sub}

    swap = {"blk": blk + (1 - 2 * hi) * 16, "sub": sub + (1 - 2 * xl) * 2}

    for i in range(16):
        for q in range(2):
            copy(factor.at[2 * i + q, :, 256 * i:256 * i + 256], blocks.at[i // 2, q, xl, core],
                 diag_send, diag_recv, beside(1 if i < 8 else -1, i % 2)).start()
    for i in range(16):
        k, row = panel_place(i, 2 * i)
        piece = factor.at[2 * i:32, :, 256 * i:256 * i + 256]
        place = pan.at[k, row:row + 32 - 2 * i, core]
        pltpu.make_async_copy(piece, place, pan_local.at[i]).start()
        copy(piece, place, pan_send.at[i], pan_recv.at[i], mate).start()

    onehot = (slots[...] == lax.broadcasted_iota(jnp.int32, (32, 32), 0)).astype(F32).astype(BF16)

    def pick(v):
        return lax.dot_general(onehot, v, NN, preferred_element_type=F32)

    for g in range(16):
        value = integrals[:, 384 * g:384 * g + 384]
        high = value.astype(BF16)
        rest = value - high.astype(F32)
        mid = rest.astype(BF16)
        low = (rest - mid.astype(F32)).astype(BF16)
        picked = pick(high) + (pick(mid) + pick(low))
        for k in range(4):
            sb[4 * g + k] = picked[:, 96 * k:96 * k + 96]

    def spread(k, _):
        to = (blk + k) % 32
        for c in range(2):
            copy(sb.at[2 * to + c], rhs.at[2 * blk + core], a_send, a_recv,
                 {"blk": to, "sub": 2 * xl + c}).start()
        return 0

    lax.fori_loop(1, 32, spread, 0)
    copy(sb.at[2 * blk + 1 - core], rhs.at[2 * blk + core], a_send, a_recv, mate).start()
    rhs[2 * blk + core] = sb[2 * blk + core]

    for i in range(16):
        k, row = panel_place(i, 2 * i)
        piece = pan.at[k, row:row + 32 - 2 * i, core]
        pltpu.make_async_copy(piece, piece, pan_local.at[i]).wait()
        copy(piece, piece, pan_send.at[i], pan_recv.at[i], mate).wait_recv()
    copy(blocks.at[0:4], blocks.at[0:4], diag_send, diag_recv, mate).wait_recv()

    def place_own(j, _):
        k, row = panel_place(2 * j + core, 2 * (2 * j + core))
        for q in range(2):
            blocks[j, q, xl] = pan[k, row + q]
        return 0

    lax.fori_loop(0, 8, place_own, 0)

    row = lax.broadcasted_iota(jnp.int32, (128, 128), 0)
    col = lax.broadcasted_iota(jnp.int32, (128, 128), 1)

    def invert(g, _):
        def block(n):
            q = n % 2
            return blocks[2 * g + n // 2, q, :, :, :, 128 * q:128 * q + 128].reshape(128, 128)

        for n in range(4):
            value = block(n)
            diag = jnp.where(row == col, value, 0.0)
            down = 1.0 / jnp.sum(diag, axis=1, keepdims=True)
            across = 1.0 / jnp.sum(diag, axis=0, keepdims=True)
            below = (row == col + 1) & (row % 2 == 1)
            half_inv[4 * g + n] = jnp.where(row == col, down, 0.0) - jnp.where(below, value * down * across, 0.0)
        size = 2
        while size < 128:
            below = (row // size == col // size + 1) & (row // (2 * size) == col // (2 * size))
            for n in range(4):
                part = jnp.where(below, block(n), 0.0)
                half_tmp[n] = dot3(split(part), split(half_inv[4 * g + n]), NN)
            for n in range(4):
                now = half_inv[4 * g + n]
                half_inv[4 * g + n] = now - dot3(split(now), split(half_tmp[n]), NN)
            size *= 2
        for n in range(2):
            lower = blocks[2 * g + n, 1, :, :, :, 0:128].reshape(128, 128)
            half_tmp[n] = dot3(split(lower), split(half_inv[4 * g + 2 * n]), NN)
        for n in range(2):
            i = 2 * (2 * g + n) + core
            dinv[i, 0:128, 0:128] = half_inv[4 * g + 2 * n]
            dinv[i, 128:256, 128:256] = half_inv[4 * g + 2 * n + 1]
            dinv[i, 0:128, 128:256] = jnp.zeros((128, 128), F32)
            dinv[i, 128:256, 0:128] = -dot3(split(half_inv[4 * g + 2 * n + 1]), split(half_tmp[n]), NN)
        return 0

    lax.fori_loop(0, 4, invert, 0)

    def share(j, _):
        copy(dinv.at[2 * j + core], dinv.at[2 * j + core], inv_send, inv_recv, mate).start()
        return 0

    lax.fori_loop(0, 8, share, 0)
    copy(rhs.at[0:63], rhs.at[0:63], a_send, a_recv, mate).wait_recv()
    copy(dinv.at[0:8], dinv.at[0:8], inv_send, inv_recv, mate).wait_recv()

    def offer(i, value):
        gbuf[i, :, xl] = value.reshape(2, 64, 96)
        copy(gbuf.at[i, :, xl], gbuf.at[i, :, xl], g_send.at[i], g_recv.at[i], peer).start()

    def factor_part(i, t):
        k, at = panel_place(i, 2 * t)
        return split(pan[k, pl.ds(at, 2)].reshape(128, 256))

    def own_out(i):
        half = rowbuf.at[y, i, 1 - core]
        copy(half, half, x_send, x_recv.at[i], mate).wait_recv()
        for k, offset in enumerate((1, -1)):
            copy(rowbuf.at[y, i], rowbuf.at[y, i], y_send.at[k, i], y_recv.at[k, i], y_at(offset)).start()

        @pl.when(same)
        def _():
            for k, offset in enumerate((1, -1)):
                copy(rowbuf.at[y, i], colbuf.at[z, i], z_send.at[k, i], z_recv.at[k, i], z_at(offset)).start()
            colbuf[z, i] = rowbuf[y, i]

        @pl.when(jnp.logical_not(same))
        def _():
            copy(rowbuf.at[y, i], colbuf.at[z, i], s_send.at[i], s_recv.at[i], swap).start()

    def swapped_out(i):
        @pl.when(jnp.logical_not(same))
        def _():
            copy(colbuf.at[z, i], colbuf.at[z, i], s_send.at[i], s_recv.at[i], swap).wait_recv()
            for k, offset in enumerate((1, -1)):
                copy(colbuf.at[z, i], colbuf.at[z, i], z_send.at[k, i], z_recv.at[k, i], z_at(offset)).start()

    def got(buf, send, recv, place, k, i):
        copy(buf.at[place, i], buf.at[place, i], send.at[k, i], recv.at[k, i], mate).wait_recv()

    def forward(i):
        odd = i % 2
        step = 1 - 2 * odd
        src = (y - step + 4) % 4
        got(rowbuf, y_send, y_recv, src, odd, i)
        copy(rowbuf.at[src, i], rowbuf.at[src, i], y_send.at[2, i], y_recv.at[2, i], y_at(step)).start()
        src = (z - step + 4) % 4
        got(colbuf, z_send, z_recv, src, odd, i)
        copy(colbuf.at[src, i], colbuf.at[src, i], z_send.at[2, i], z_recv.at[2, i], z_at(step)).start()

    def whole(buf, k, c):
        return jnp.concatenate([buf[k, 2 * c].reshape(192, 128), buf[k, 2 * c + 1].reshape(192, 128)], axis=1)

    def arrived(c):
        for odd in range(2):
            i = 2 * c + odd
            step = 1 - 2 * odd
            got(rowbuf, y_send, y_recv, (y + step + 4) % 4, 1 - odd, i)
            got(colbuf, z_send, z_recv, (z + step + 4) % 4, 1 - odd, i)
            got(rowbuf, y_send, y_recv, (y + 2) % 4, 2, i)
            got(colbuf, z_send, z_recv, (z + 2) % 4, 2, i)
        for k in range(4):
            high, low = split(whole(colbuf, k, c))
            colh[k * 192:k * 192 + 192] = high
            coll[k * 192:k * 192 + 192] = low

    def product_rows(c, k):
        acc[k] = acc[k] + dot3(split(whole(rowbuf, k, c)), (colh[...], coll[...]), NT)

    def product(c):
        arrived(c)

        def part(k, _):
            product_rows(c, k)
            return 0

        lax.fori_loop(0, 4, part, 0)

    acc[...] = jnp.zeros_like(acc)
    offer(0, rhs[0:4].reshape(128, 96))

    def round_of(i, _):
        inverse = split(dinv[i])

        @pl.when(i > 0)
        def _():
            def later(t, _):
                term = dot3(factor_part(i - 1, t), (xh[...], xlow[...]), NN)
                rows = pl.ds(4 * t, 4)
                rhs[rows] = rhs[rows] - term.reshape(4, 32, 96)
                return 0

            lax.fori_loop(i + 1, 16, later, 0)
            own_out(i - 1)

        @pl.when(i > 1)
        def _():
            swapped_out(i - 2)

        @pl.when(i > 3)
        def _():
            forward(i - 4)

        @pl.when((i > 6) & (i % 2 == 1))
        def _():
            product((i - 7) // 2)

        other = gbuf.at[i, :, 1 - xl]
        copy(other, other, g_send.at[i], g_recv.at[i], peer).wait_recv()
        solved = dot3(inverse, split(gbuf[i].reshape(256, 96)), NN)
        high, low = split(solved)
        xh[...] = high
        xlow[...] = low

        @pl.when(i < 15)
        def _():
            term = dot3(factor_part(i, i + 1), (high, low), NN)
            offer(i + 1, rhs[pl.ds(4 * i + 4, 4)].reshape(128, 96) - term)

        xbuf[...] = solved.reshape(2, 128, 96)
        tx[i] = xbuf[1 - core].T
        copy(tx.at[i], rowbuf.at[y, i, core], x_send, x_recv.at[i], mate).start()
        rowbuf[y, i, core] = xbuf[core].T
        return 0

    lax.fori_loop(0, 16, round_of, 0)

    own_out(15)
    swapped_out(14)
    forward(12)
    forward(13)
    swapped_out(15)
    product(5)
    forward(14)
    product(6)
    forward(15)
    arrived(7)

    mine = pl.ds(pl.multiple_of(core * 384, 128), 384)
    theirs = pl.ds(pl.multiple_of((1 - core) * 384, 128), 384)
    order = [(y + 2) % 4, (y + 1) % 4, (y + 3) % 4, y]

    def trade(n):
        k = order[n]
        return copy(acc.at[k, :, theirs], exch.at[k], t_send.at[n], t_recv.at[n], mate)

    for n in range(4):
        product_rows(7, order[n])
        trade(n).start()

    def summed(n):
        trade(n).wait_recv()
        k = order[n]
        total[k] = acc[k, :, mine] + exch[k]

    summed(0)
    hops = []
    for at, offset in enumerate((1, -1)):
        hops.append(copy(total.at[order[0], 96 * at:96 * at + 96], relay.at[at],
                         e_send.at[at], e_recv.at[at], y_at(offset)))
        hops[-1].start()
    for n, offset in ((1, 1), (2, -1)):
        summed(n)
        hops.append(copy(total.at[order[n]], final.at[y], e_send.at[n + 1], e_recv.at[n + 1], y_at(offset)))
        hops[-1].start()
    for at, offset in enumerate((1, -1)):
        copy(relay.at[at], relay.at[at], e_send.at[at], e_recv.at[at], mate).wait_recv()
        src = (y - offset + 4) % 4
        hops.append(copy(relay.at[at], final.at[src, 96 * at:96 * at + 96],
                         e_send.at[4 + at], e_recv.at[4 + at], y_at(offset)))
        hops[-1].start()
    summed(3)
    final[y] = total[y]
    for n, offset in ((1, 1), (2, -1)):
        src = (y - offset + 4) % 4
        copy(final.at[src], final.at[src], e_send.at[n + 1], e_recv.at[n + 1], mate).wait_recv()
    src = (y + 2) % 4
    for at in range(2):
        piece = final.at[src, 96 * at:96 * at + 96]
        copy(piece, piece, e_send.at[4 + at], e_recv.at[4 + at], mate).wait_recv()
    for k in range(2):
        for q in range(4):
            place = (k * 4 + q) * 192
            out[:, place:place + 192] = final[q, :, k * 192:k * 192 + 192]
    for hop in hops:
        hop.wait_send()
    for n in range(4):
        trade(n).wait_send()

    def drain(i, _):
        piece = rowbuf.at[y, i]
        for k in range(3):
            copy(piece, piece, y_send.at[k, i], y_recv.at[k, i], mate).wait_send()
            copy(piece, piece, z_send.at[k, i], z_recv.at[k, i], mate).wait_send()

        @pl.when(jnp.logical_not(same))
        def _():
            copy(piece, piece, s_send.at[i], s_recv.at[i], swap).wait_send()

        return 0

    lax.fori_loop(0, 16, drain, 0)

    for i in range(16):
        k, row = panel_place(i, 2 * i)
        piece = pan.at[k, row:row + 32 - 2 * i, core]
        copy(piece, piece, pan_send.at[i], pan_recv.at[i], mate).wait_send()
        mine = gbuf.at[i, :, xl]
        copy(mine, mine, g_send.at[i], g_recv.at[i], peer).wait_send()
    copy(blocks.at[0:4], blocks.at[0:4], diag_send, diag_recv, mate).wait_send()
    copy(sb.at[0:63], sb.at[0:63], a_send, a_recv, mate).wait_send()
    copy(dinv.at[0:8], dinv.at[0:8], inv_send, inv_recv, mate).wait_send()
    copy(tx, tx, x_send, x_recv.at[0], mate).wait_send()


def coulomb_block(integrals, slots, factor):
    dma = pltpu.SemaphoreType.DMA
    vmem = pl.BlockSpec(memory_space=pltpu.VMEM)
    return pl.pallas_call(
        fused_kernel,
        out_shape=jax.ShapeDtypeStruct((192, 1536), F32),
        in_specs=[vmem, vmem, pl.BlockSpec(memory_space=pl.ANY)],
        out_specs=vmem,
        scratch_shapes=[
            pltpu.VMEM((8, 34, 2, 32, 256), F32),
            pltpu.VMEM((8, 2, 2, 2, 32, 256), F32),
            pltpu.VMEM((16, 128, 128), F32),
            pltpu.VMEM((4, 128, 128), F32),
            pltpu.VMEM((16, 256, 256), F32),
            pltpu.VMEM((64, 32, 96), F32),
            pltpu.VMEM((64, 32, 96), F32),
            pltpu.VMEM((16, 2, 2, 64, 96), F32),
            pltpu.VMEM((256, 96), BF16),
            pltpu.VMEM((256, 96), BF16),
            pltpu.VMEM((2, 128, 96), F32),
            pltpu.VMEM((16, 96, 128), F32),
            pltpu.VMEM((4, 16, 2, 96, 128), F32),
            pltpu.VMEM((4, 16, 2, 96, 128), F32),
            pltpu.VMEM((4, 192, 768), F32),
            pltpu.VMEM((768, 256), BF16),
            pltpu.VMEM((768, 256), BF16),
            pltpu.VMEM((4, 192, 384), F32),
            pltpu.VMEM((4, 192, 384), F32),
            pltpu.VMEM((4, 192, 384), F32),
            pltpu.VMEM((2, 96, 384), F32),
            dma((16,)), dma((16,)), dma((16,)), dma, dma, dma, dma, dma, dma,
            dma((16,)), dma((16,)), dma, dma((16,)),
            dma((3, 16)), dma((3, 16)), dma((3, 16)), dma((3, 16)), dma((16,)), dma((16,)),
            dma((4,)), dma((4,)), dma((6,)), dma((6,)),
        ],
        compiler_params=pltpu.CompilerParams(
            has_side_effects=True, vmem_limit_bytes=60 * 2**20),
    )(integrals, slots, factor)


def shards(integrals, slot_order, factor_rows, occ_energy, slab_index, virt_energy):
    coulomb = coulomb_block(integrals[0, 0], slot_order[0], factor_rows[:, 0])
    pair_rows, quarter = coulomb.shape
    slab_start = slab_index[0] * NOCC
    occ_slab = lax.dynamic_slice_in_dim(occ_energy, slab_start, NOCC)
    pair_energy = jnp.repeat(occ_slab, NVIRT) - jnp.tile(virt_energy, NOCC)
    row_energy = lax.dynamic_slice_in_dim(pair_energy, lax.axis_index("blk") * pair_rows, pair_rows)
    col_energy = lax.dynamic_slice_in_dim(pair_energy, lax.axis_index("sub") * quarter, quarter)
    return coulomb / (row_energy[:, None] + col_energy[None, :])


def solution(mesh):
    in_specs = (
        P("blk", "sub", None, None),
        P("blk", "sub", None),
        P(None, "sub", None, None),
        P(),
        P(),
        P(),
    )
    out_specs = P("blk", "sub")
    return jax.shard_map(shards, mesh=mesh, in_specs=in_specs, out_specs=out_specs, check_vma=False)
```

time: 202 us -> 155 us (0.77)
  Pallas kernels: 196 us -> 148 us
    pallas_call x2 -> x1, Pallas kernels: 196 us -> 148 us  [coulomb_block(): pl.pallas_call(fused_kernel, out_shape=jax.ShapeDtypeStruct((192, 1536),...]
where the time goes in v3:
time: 155 us; the launch traced here: 153 us
  Pallas kernels  148 us (95%)
  other arithmetic  3.28 us (2%)
    pallas_call x1, Pallas kernels, coulomb_block(): pl.pallas_call(fused_kernel, out_shape=jax.ShapeDtypeStruct((192, 1536),...  148 us

profile of v3, /device:TPU:5, one launch (start us, length us, event | category | flops | bytes accessed | tf_op | source)
XLA Modules:
  0.0 153.1 jit_solution(879960662110375098)
XLA Ops:
  0.7 0.8 dynamic_slice.9
  1.4 0.8 broadcast_subtract_fusion
  2.2 0.1 dynamic_slice.10
  2.3 0.1 dynamic_slice.11
  2.4 148.3 %shard_map.64 = f32[192,1536]{1,0:T(8,128)} custom-call(f32[32,6144]{1,0:T(8,128)} %bitcast.5, s32[1,32]{1,0:T(1,128)} %bitcast.6, f32[32,32,4096]{2,1,0:T(8,128)} %bitcast.4), custom_call_target="tpu_custom_call" | custom-call | tf_op jit(solution)/shard_map/pallas_call | solution.py:380
  150.6 2.5 %add_divide_fusion = f32[192,1536]{1,0:T(8,128)} fusion(f32[192,1536]{1,0:T(8,128)} %shard_map.64, f32[1536]{0:T(1024)S(1)} %dynamic_slice.11, f32[192]{0:T(256)S(1)} %dynamic_slice.10), kind=kLoop, calls=%fused_computation | loop fusion | flops 589824 | bytes 2366208 | tf_op jit(solution)/shard_map/div | solution.py:425
  (1 shorter events, 0.0 us)

commit v4 on v3

--- a/solution.py
+++ b/solution.py
@@ -7,9 +7,7 @@
 from jax.experimental.pallas import tpu as pltpu
 from jax.sharding import PartitionSpec as P
 
-NVIRT = 2048
 NOCC = 3
-PRECISE = lax.Precision.HIGHEST
 F32 = jnp.float32
 BF16 = jnp.bfloat16
 MESH = pl.DeviceIdType.MESH
@@ -41,8 +39,8 @@
     return jnp.where(i < 8, i, 15 - i), jnp.where(i < 8, r - 2 * i, r + 2)
 
 
-def fused_kernel(integrals, slots, factor, out, pan, blocks, half_inv, half_tmp, dinv, sb, rhs, gbuf,
-                 xh, xlow, xbuf, tx, rowbuf, colbuf, acc, colh, coll, exch, total, final, relay,
+def fused_kernel(integrals, slots, factor, occ, slab, virt, out, pan, blocks, half_inv, half_tmp, dinv, sb, rhs, gbuf,
+                 xh, xlow, xbuf, tx, rowbuf, colbuf, acc, cols, colh, coll, pairs, exch, total, final, relay,
                  pan_local, pan_send, pan_recv, diag_send, diag_recv, a_send, a_recv,
                  inv_send, inv_recv, g_send, g_recv, x_send, x_recv,
                  y_send, y_recv, z_send, z_recv, s_send, s_recv, t_send, t_recv, e_send, e_recv):
@@ -67,16 +65,31 @@
 
     swap = {"blk": blk + (1 - 2 * hi) * 16, "sub": sub + (1 - 2 * xl) * 2}
 
-    for i in range(16):
+    barrier = pltpu.get_barrier_semaphore()
+
+    def greet(k, _):
+        for c in range(2):
+            pl.semaphore_signal(barrier, inc=1, device_id_type=MESH,
+                                device_id={"blk": (blk + k) % 32, "sub": 2 * xl + c})
+        return 0
+
+    lax.fori_loop(1, 32, greet, 0)
+    pl.semaphore_signal(barrier, inc=1, device_id=mate, device_id_type=MESH)
+    for offset in (1, -1):
+        for c in range(2):
+            pl.semaphore_signal(barrier, inc=1, device_id=beside(offset, c), device_id_type=MESH)
+
+    def slab_of(i, q):
+        wide = 128 * (q + 1)
+        return factor.at[2 * i + q, :, pl.ds(pl.multiple_of(256 * i, 256), wide)]
+
+    def slab_place(j, q, at_core):
+        return blocks.at[j, q, xl, at_core, :, 0:128 * (q + 1)]
+
+    order = (0, 1, 4, 5, 2, 3, 6, 7)
+    for j in order:
         for q in range(2):
-            copy(factor.at[2 * i + q, :, 256 * i:256 * i + 256], blocks.at[i // 2, q, xl, core],
-                 diag_send, diag_recv, beside(1 if i < 8 else -1, i % 2)).start()
-    for i in range(16):
-        k, row = panel_place(i, 2 * i)
-        piece = factor.at[2 * i:32, :, 256 * i:256 * i + 256]
-        place = pan.at[k, row:row + 32 - 2 * i, core]
-        pltpu.make_async_copy(piece, place, pan_local.at[i]).start()
-        copy(piece, place, pan_send.at[i], pan_recv.at[i], mate).start()
+            pltpu.make_async_copy(slab_of(2 * j + core, q), slab_place(j, q, core), diag_recv.at[q, j // 2]).start()
 
     onehot = (slots[...] == lax.broadcasted_iota(jnp.int32, (32, 32), 0)).astype(F32).astype(BF16)
 
@@ -93,6 +106,16 @@
         for k in range(4):
             sb[4 * g + k] = picked[:, 96 * k:96 * k + 96]
 
+    pl.semaphore_wait(barrier, 67)
+
+    for j in order:
+        for q in range(2):
+            for c in range(2):
+                copy(slab_of(2 * j + c, q), slab_place(j, q, core), diag_send.at[q], diag_recv.at[q, j // 2],
+                     beside(1 if j < 4 else -1, c)).start()
+            copy(slab_of(2 * j + 1 - core, q), slab_place(j, q, core), diag_send.at[q], diag_recv.at[q, j // 2],
+                 mate).start()
+
     def spread(k, _):
         to = (blk + k) % 32
         for c in range(2):
@@ -106,23 +129,23 @@
 
     for i in range(16):
         k, row = panel_place(i, 2 * i)
-        piece = pan.at[k, row:row + 32 - 2 * i, core]
-        pltpu.make_async_copy(piece, piece, pan_local.at[i]).wait()
-        copy(piece, piece, pan_send.at[i], pan_recv.at[i], mate).wait_recv()
-    copy(blocks.at[0:4], blocks.at[0:4], diag_send, diag_recv, mate).wait_recv()
-
-    def place_own(j, _):
-        k, row = panel_place(2 * j + core, 2 * (2 * j + core))
-        for q in range(2):
-            blocks[j, q, xl] = pan[k, row + q]
-        return 0
-
-    lax.fori_loop(0, 8, place_own, 0)
+        piece = factor.at[2 * i:32, :, 256 * i:256 * i + 256]
+        place = pan.at[k, row:row + 32 - 2 * i, core]
+        pltpu.make_async_copy(piece, place, pan_local.at[i]).start()
+        copy(piece, place, pan_send.at[i], pan_recv.at[i], mate).start()
+
+    for t in range(12):
+        pairs[:, 512 * t:512 * t + 512] = occ[slab[0] * NOCC + t // 4] - virt[:, 512 * (t % 4):512 * (t % 4) + 512]
 
     row = lax.broadcasted_iota(jnp.int32, (128, 128), 0)
     col = lax.broadcasted_iota(jnp.int32, (128, 128), 1)
 
-    def invert(g, _):
+    def invert(turn, _):
+        g = (turn % 2) * 2 + turn // 2
+        for q in range(2):
+            piece = blocks.at[pl.ds(2 * g, 2), q, :, :, :, 0:128 * (q + 1)]
+            pltpu.make_async_copy(piece, piece, diag_recv.at[q, g]).wait()
+
         def block(n):
             q = n % 2
             return blocks[2 * g + n // 2, q, :, :, :, 128 * q:128 * q + 128].reshape(128, 128)
@@ -153,17 +176,14 @@
             dinv[i, 128:256, 128:256] = half_inv[4 * g + 2 * n + 1]
             dinv[i, 0:128, 128:256] = jnp.zeros((128, 128), F32)
             dinv[i, 128:256, 0:128] = -dot3(split(half_inv[4 * g + 2 * n + 1]), split(half_tmp[n]), NN)
+        for n in range(2):
+            i = 2 * (2 * g + n) + core
+            copy(dinv.at[i], dinv.at[i], inv_send, inv_recv.at[g], mate).start()
         return 0
 
     lax.fori_loop(0, 4, invert, 0)
 
-    def share(j, _):
-        copy(dinv.at[2 * j + core], dinv.at[2 * j + core], inv_send, inv_recv, mate).start()
-        return 0
-
-    lax.fori_loop(0, 8, share, 0)
     copy(rhs.at[0:63], rhs.at[0:63], a_send, a_recv, mate).wait_recv()
-    copy(dinv.at[0:8], dinv.at[0:8], inv_send, inv_recv, mate).wait_recv()
 
     def offer(i, value):
         gbuf[i, :, xl] = value.reshape(2, 64, 96)
@@ -221,12 +241,14 @@
             got(rowbuf, y_send, y_recv, (y + 2) % 4, 2, i)
             got(colbuf, z_send, z_recv, (z + 2) % 4, 2, i)
         for k in range(4):
-            high, low = split(whole(colbuf, k, c))
-            colh[k * 192:k * 192 + 192] = high
-            coll[k * 192:k * 192 + 192] = low
+            cols[k * 192:k * 192 + 192] = whole(colbuf, k, c)
+        for m in range(6):
+            high, low = split(cols[128 * m:128 * m + 128].T)
+            colh[:, 128 * m:128 * m + 128] = high
+            coll[:, 128 * m:128 * m + 128] = low
 
     def product_rows(c, k):
-        acc[k] = acc[k] + dot3(split(whole(rowbuf, k, c)), (colh[...], coll[...]), NT)
+        acc[k] = acc[k] + dot3(split(whole(rowbuf, k, c)), (colh[...], coll[...]), NN)
 
     def product(c):
         arrived(c)
@@ -238,20 +260,31 @@
         lax.fori_loop(0, 4, part, 0)
 
     acc[...] = jnp.zeros_like(acc)
+    for i in range(16):
+        k, row = panel_place(i, 2 * i)
+        piece = pan.at[k, row:row + 32 - 2 * i, core]
+        pltpu.make_async_copy(piece, piece, pan_local.at[i]).wait()
+        copy(piece, piece, pan_send.at[i], pan_recv.at[i], mate).wait_recv()
     offer(0, rhs[0:4].reshape(128, 96))
 
     def round_of(i, _):
+        @pl.when(i % 4 == 0)
+        def _():
+            copy(dinv.at[0:2], dinv.at[0:2], inv_send, inv_recv.at[i // 4], mate).wait_recv()
+
         inverse = split(dinv[i])
 
         @pl.when(i > 0)
         def _():
-            def later(t, _):
-                term = dot3(factor_part(i - 1, t), (xh[...], xlow[...]), NN)
-                rows = pl.ds(4 * t, 4)
-                rhs[rows] = rhs[rows] - term.reshape(4, 32, 96)
+            def later(u, _):
+                k, at = panel_place(i - 1, 4 * u)
+                part = split(pan[k, pl.ds(at, 4)].reshape(256, 256))
+                term = dot3(part, (xh[...], xlow[...]), NN)
+                rows = pl.ds(8 * u, 8)
+                rhs[rows] = rhs[rows] - term.reshape(8, 32, 96)
                 return 0
 
-            lax.fori_loop(i + 1, 16, later, 0)
+            lax.fori_loop((i + 1) // 2, 8, later, 0)
             own_out(i - 1)
 
         @pl.when(i > 1)
@@ -299,7 +332,7 @@
 
     mine = pl.ds(pl.multiple_of(core * 384, 128), 384)
     theirs = pl.ds(pl.multiple_of((1 - core) * 384, 128), 384)
-    order = [(y + 2) % 4, (y + 1) % 4, (y + 3) % 4, y]
+    order = ((y + 2) % 4, (y + 1) % 4, (y + 3) % 4, y)
 
     def trade(n):
         k = order[n]
@@ -339,10 +372,15 @@
     for at in range(2):
         piece = final.at[src, 96 * at:96 * at + 96]
         copy(piece, piece, e_send.at[4 + at], e_recv.at[4 + at], mate).wait_recv()
+    window = pairs[:, pl.ds(pl.multiple_of((blk * 192) // 128 * 128, 128), 256)]
+    across = jnp.where(blk % 2 == 1, window[:, 64:256], window[:, 0:192])
+    line = lax.broadcasted_iota(jnp.int32, (192, 192), 0)
+    lane = lax.broadcasted_iota(jnp.int32, (192, 192), 1)
+    down = jnp.sum(jnp.where(line == lane, across, 0.0), axis=1, keepdims=True)
     for k in range(2):
-        for q in range(4):
-            place = (k * 4 + q) * 192
-            out[:, place:place + 192] = final[q, :, k * 192:k * 192 + 192]
+        wide = pairs[:, pl.ds(pl.multiple_of(sub * 1536 + k * 768, 128), 768)]
+        sums = jnp.concatenate([final[q, :, k * 192:k * 192 + 192] for q in range(4)], axis=1)
+        out[:, k * 768:k * 768 + 768] = sums / (down + wide)
     for hop in hops:
         hop.wait_send()
     for n in range(4):
@@ -368,19 +406,22 @@
         copy(piece, piece, pan_send.at[i], pan_recv.at[i], mate).wait_send()
         mine = gbuf.at[i, :, xl]
         copy(mine, mine, g_send.at[i], g_recv.at[i], peer).wait_send()
-    copy(blocks.at[0:4], blocks.at[0:4], diag_send, diag_recv, mate).wait_send()
+    for q in range(2):
+        piece = blocks.at[0:6, q, :, :, :, 0:128 * (q + 1)]
+        copy(piece, piece, diag_send.at[q], diag_recv.at[q, 0], mate).wait_send()
     copy(sb.at[0:63], sb.at[0:63], a_send, a_recv, mate).wait_send()
-    copy(dinv.at[0:8], dinv.at[0:8], inv_send, inv_recv, mate).wait_send()
+    copy(dinv.at[0:8], dinv.at[0:8], inv_send, inv_recv.at[0], mate).wait_send()
     copy(tx, tx, x_send, x_recv.at[0], mate).wait_send()
 
 
-def coulomb_block(integrals, slots, factor):
+def amplitude_block(integrals, slots, factor, occ, slab, virt):
     dma = pltpu.SemaphoreType.DMA
     vmem = pl.BlockSpec(memory_space=pltpu.VMEM)
+    smem = pl.BlockSpec(memory_space=pltpu.SMEM)
     return pl.pallas_call(
         fused_kernel,
         out_shape=jax.ShapeDtypeStruct((192, 1536), F32),
-        in_specs=[vmem, vmem, pl.BlockSpec(memory_space=pl.ANY)],
+        in_specs=[vmem, vmem, pl.BlockSpec(memory_space=pl.ANY), smem, smem, vmem],
         out_specs=vmem,
         scratch_shapes=[
             pltpu.VMEM((8, 34, 2, 32, 256), F32),
@@ -398,31 +439,27 @@
             pltpu.VMEM((4, 16, 2, 96, 128), F32),
             pltpu.VMEM((4, 16, 2, 96, 128), F32),
             pltpu.VMEM((4, 192, 768), F32),
-            pltpu.VMEM((768, 256), BF16),
-            pltpu.VMEM((768, 256), BF16),
+            pltpu.VMEM((768, 256), F32),
+            pltpu.VMEM((256, 768), BF16),
+            pltpu.VMEM((256, 768), BF16),
+            pltpu.VMEM((1, 6144), F32),
             pltpu.VMEM((4, 192, 384), F32),
             pltpu.VMEM((4, 192, 384), F32),
             pltpu.VMEM((4, 192, 384), F32),
             pltpu.VMEM((2, 96, 384), F32),
-            dma((16,)), dma((16,)), dma((16,)), dma, dma, dma, dma, dma, dma,
+            dma((16,)), dma((16,)), dma((16,)), dma((2,)), dma((2, 4)), dma, dma, dma, dma((4,)),
             dma((16,)), dma((16,)), dma, dma((16,)),
             dma((3, 16)), dma((3, 16)), dma((3, 16)), dma((3, 16)), dma((16,)), dma((16,)),
             dma((4,)), dma((4,)), dma((6,)), dma((6,)),
         ],
         compiler_params=pltpu.CompilerParams(
-            has_side_effects=True, vmem_limit_bytes=60 * 2**20),
-    )(integrals, slots, factor)
+            collective_id=0, has_side_effects=True, vmem_limit_bytes=60 * 2**20),
+    )(integrals, slots, factor, occ, slab, virt)
 
 
 def shards(integrals, slot_order, factor_rows, occ_energy, slab_index, virt_energy):
-    coulomb = coulomb_block(integrals[0, 0], slot_order[0], factor_rows[:, 0])
-    pair_rows, quarter = coulomb.shape
-    slab_start = slab_index[0] * NOCC
-    occ_slab = lax.dynamic_slice_in_dim(occ_energy, slab_start, NOCC)
-    pair_energy = jnp.repeat(occ_slab, NVIRT) - jnp.tile(virt_energy, NOCC)
-    row_energy = lax.dynamic_slice_in_dim(pair_energy, lax.axis_index("blk") * pair_rows, pair_rows)
-    col_energy = lax.dynamic_slice_in_dim(pair_energy, lax.axis_index("sub") * quarter, quarter)
-    return coulomb / (row_energy[:, None] + col_energy[None, :])
+    return amplitude_block(integrals[0, 0], slot_order[0], factor_rows[:, 0],
+                           occ_energy, slab_index, virt_energy[None])
 
 
 def solution(mesh):

time: 155 us -> 137 us (0.88)
  Pallas kernels: 148 us -> 133 us
  other arithmetic: 3.28 us -> 0 us
    pallas_call x1, Pallas kernels: 148 us -> 133 us  [amplitude_block(): pl.pallas_call(fused_kernel, out_shape=jax.ShapeDtypeStruct((192, 1536),...]
    div x1 -> x0, other arithmetic: 2.51 us -> none  [shards(): return coulomb / (row_energy[:, None] + col_energy[None, :])]
    unnamed x0 -> x1, local copies, waits for them, and re-layouts: none -> 2.36 us
where the time goes in v4:
time: 137 us; the launch traced here: 136 us
  Pallas kernels  133 us (97%)
  local copies, waits for them, and re-layouts  2.36 us (2%)
    pallas_call x1, Pallas kernels, amplitude_block(): pl.pallas_call(fused_kernel, out_shape=jax.ShapeDtypeStruct((192, 1536),...  133 us

profile of v4, /device:TPU:5, one launch (start us, length us, event | category | flops | bytes accessed | tf_op | source)
XLA Modules:
  0.0 135.8 jit_solution(10113633301465987280)
XLA Ops:
  0.7 132.8 %shard_map.64 = f32[192,1536]{1,0:T(8,128)} custom-call(f32[32,6144]{1,0:T(8,128)} %bitcast.5, s32[1,32]{1,0:T(1,128)} %bitcast.7, f32[32,32,4096]{2,1,0:T(8,128)} %bitcast.4, f32[384]{0:T(512)} %occ.1, s32[1]{0:T(128)S(6)} %copy.8.slab, f32[1,2048]{1,0:T(1,128)} %bitcast.6), custom_call_target="tpu_custom_call" | custom-call | tf_op jit(solution)/shard_map/pallas_call | solution.py:421
  133.4 2.4 %copy.9 = f32[192,1536]{1,0:T(8,128)} copy(f32[192,1536]{1,0:T(8,128)} %shard_map.64) | data formatting | bytes 2359296

commit v5 on v4

--- a/solution.py
+++ b/solution.py
@@ -39,9 +39,9 @@
     return jnp.where(i < 8, i, 15 - i), jnp.where(i < 8, r - 2 * i, r + 2)
 
 
-def fused_kernel(integrals, slots, factor, occ, slab, virt, out, pan, blocks, half_inv, half_tmp, dinv, sb, rhs, gbuf,
+def fused_kernel(integrals, slots, factor, occ, slab_hbm, virt, out, slab, pan, blocks, half_inv, half_tmp, dinv, sb, rhs, known, gbuf,
                  xh, xlow, xbuf, tx, rowbuf, colbuf, acc, cols, colh, coll, pairs, exch, total, final, relay,
-                 pan_local, pan_send, pan_recv, diag_send, diag_recv, a_send, a_recv,
+                 in_local, pan_local, pan_send, pan_recv, diag_send, diag_recv, a_send, a_recv,
                  inv_send, inv_recv, g_send, g_recv, x_send, x_recv,
                  y_send, y_recv, z_send, z_recv, s_send, s_recv, t_send, t_recv, e_send, e_recv):
     blk, sub = lax.axis_index("blk"), lax.axis_index("sub")
@@ -65,6 +65,7 @@
 
     swap = {"blk": blk + (1 - 2 * hi) * 16, "sub": sub + (1 - 2 * xl) * 2}
 
+    pltpu.make_async_copy(slab_hbm, slab, in_local).start()
     barrier = pltpu.get_barrier_semaphore()
 
     def greet(k, _):
@@ -119,12 +120,12 @@
     def spread(k, _):
         to = (blk + k) % 32
         for c in range(2):
-            copy(sb.at[2 * to + c], rhs.at[2 * blk + core], a_send, a_recv,
+            copy(sb.at[2 * to + c], rhs.at[2 * blk + core], a_send, a_recv.at[blk // 2],
                  {"blk": to, "sub": 2 * xl + c}).start()
         return 0
 
     lax.fori_loop(1, 32, spread, 0)
-    copy(sb.at[2 * blk + 1 - core], rhs.at[2 * blk + core], a_send, a_recv, mate).start()
+    copy(sb.at[2 * blk + 1 - core], rhs.at[2 * blk + core], a_send, a_recv.at[blk // 2], mate).start()
     rhs[2 * blk + core] = sb[2 * blk + core]
 
     for i in range(16):
@@ -134,8 +135,9 @@
         pltpu.make_async_copy(piece, place, pan_local.at[i]).start()
         copy(piece, place, pan_send.at[i], pan_recv.at[i], mate).start()
 
-    for t in range(12):
-        pairs[:, 512 * t:512 * t + 512] = occ[slab[0] * NOCC + t // 4] - virt[:, 512 * (t % 4):512 * (t % 4) + 512]
+    pltpu.make_async_copy(slab_hbm, slab, in_local).wait()
+    for t in range(3):
+        pairs[:, 2048 * t:2048 * t + 2048] = occ[slab[0] * NOCC + t] - virt[...]
 
     row = lax.broadcasted_iota(jnp.int32, (128, 128), 0)
     col = lax.broadcasted_iota(jnp.int32, (128, 128), 1)
@@ -183,11 +185,18 @@
 
     lax.fori_loop(0, 4, invert, 0)
 
-    copy(rhs.at[0:63], rhs.at[0:63], a_send, a_recv, mate).wait_recv()
-
     def offer(i, value):
         gbuf[i, :, xl] = value.reshape(2, 64, 96)
         copy(gbuf.at[i, :, xl], gbuf.at[i, :, xl], g_send.at[i], g_recv.at[i], peer).start()
+
+    def right_side(i):
+        for count, here in ((3, blk // 2 == i), (4, blk // 2 != i)):
+            @pl.when(here)
+            def _(count=count):
+                piece = rhs.at[0:count]
+                copy(piece, piece, a_send, a_recv.at[i], mate).wait_recv()
+
+        return rhs[pl.ds(4 * i, 4)].reshape(128, 96)
 
     def factor_part(i, t):
         k, at = panel_place(i, 2 * t)
@@ -219,15 +228,18 @@
     def got(buf, send, recv, place, k, i):
         copy(buf.at[place, i], buf.at[place, i], send.at[k, i], recv.at[k, i], mate).wait_recv()
 
-    def forward(i):
+    def forward(buf, send, recv, me, at, i):
         odd = i % 2
         step = 1 - 2 * odd
-        src = (y - step + 4) % 4
-        got(rowbuf, y_send, y_recv, src, odd, i)
-        copy(rowbuf.at[src, i], rowbuf.at[src, i], y_send.at[2, i], y_recv.at[2, i], y_at(step)).start()
-        src = (z - step + 4) % 4
-        got(colbuf, z_send, z_recv, src, odd, i)
-        copy(colbuf.at[src, i], colbuf.at[src, i], z_send.at[2, i], z_recv.at[2, i], z_at(step)).start()
+        src = (me - step + 4) % 4
+        got(buf, send, recv, src, odd, i)
+        copy(buf.at[src, i], buf.at[src, i], send.at[2, i], recv.at[2, i], at(step)).start()
+
+    def forward_y(i):
+        forward(rowbuf, y_send, y_recv, y, y_at, i)
+
+    def forward_z(i):
+        forward(colbuf, z_send, z_recv, z, z_at, i)
 
     def whole(buf, k, c):
         return jnp.concatenate([buf[k, 2 * c].reshape(192, 128), buf[k, 2 * c + 1].reshape(192, 128)], axis=1)
@@ -250,14 +262,12 @@
     def product_rows(c, k):
         acc[k] = acc[k] + dot3(split(whole(rowbuf, k, c)), (colh[...], coll[...]), NN)
 
-    def product(c):
-        arrived(c)
-
+    def product_half(c, half):
         def part(k, _):
             product_rows(c, k)
             return 0
 
-        lax.fori_loop(0, 4, part, 0)
+        lax.fori_loop(2 * half, 2 * half + 2, part, 0)
 
     acc[...] = jnp.zeros_like(acc)
     for i in range(16):
@@ -265,7 +275,8 @@
         piece = pan.at[k, row:row + 32 - 2 * i, core]
         pltpu.make_async_copy(piece, piece, pan_local.at[i]).wait()
         copy(piece, piece, pan_send.at[i], pan_recv.at[i], mate).wait_recv()
-    offer(0, rhs[0:4].reshape(128, 96))
+    known[...] = jnp.zeros_like(known)
+    offer(0, right_side(0))
 
     def round_of(i, _):
         @pl.when(i % 4 == 0)
@@ -281,7 +292,7 @@
                 part = split(pan[k, pl.ds(at, 4)].reshape(256, 256))
                 term = dot3(part, (xh[...], xlow[...]), NN)
                 rows = pl.ds(8 * u, 8)
-                rhs[rows] = rhs[rows] - term.reshape(8, 32, 96)
+                known[rows] = known[rows] + term.reshape(8, 32, 96)
                 return 0
 
             lax.fori_loop((i + 1) // 2, 8, later, 0)
@@ -291,13 +302,26 @@
         def _():
             swapped_out(i - 2)
 
-        @pl.when(i > 3)
-        def _():
-            forward(i - 4)
-
-        @pl.when((i > 6) & (i % 2 == 1))
-        def _():
-            product((i - 7) // 2)
+        @pl.when((i > 5) & (i % 2 == 0))
+        def _():
+            arrived((i - 6) // 2)
+
+        @pl.when(i > 5)
+        def _():
+            product_half((i - 6) // 2, i % 2)
+
+        @pl.when(i > 1)
+        def _():
+            forward_y(i - 2)
+
+        @pl.when(i > 2)
+        def _():
+            forward_z(i - 3)
+
+        @pl.when(i < 15)
+        def _():
+            rest = right_side(i + 1) - known[pl.ds(4 * i + 4, 4)].reshape(128, 96)
+            rhs[pl.ds(4 * i + 4, 4)] = rest.reshape(4, 32, 96)
 
         other = gbuf.at[i, :, 1 - xl]
         copy(other, other, g_send.at[i], g_recv.at[i], peer).wait_recv()
@@ -321,13 +345,18 @@
 
     own_out(15)
     swapped_out(14)
-    forward(12)
-    forward(13)
+    forward_y(14)
+    forward_z(13)
     swapped_out(15)
-    product(5)
-    forward(14)
-    product(6)
-    forward(15)
+    arrived(5)
+    product_half(5, 0)
+    forward_z(14)
+    forward_y(15)
+    product_half(5, 1)
+    arrived(6)
+    product_half(6, 0)
+    forward_z(15)
+    product_half(6, 1)
     arrived(7)
 
     mine = pl.ds(pl.multiple_of(core * 384, 128), 384)
@@ -409,7 +438,7 @@
     for q in range(2):
         piece = blocks.at[0:6, q, :, :, :, 0:128 * (q + 1)]
         copy(piece, piece, diag_send.at[q], diag_recv.at[q, 0], mate).wait_send()
-    copy(sb.at[0:63], sb.at[0:63], a_send, a_recv, mate).wait_send()
+    copy(sb.at[0:63], sb.at[0:63], a_send, a_recv.at[0], mate).wait_send()
     copy(dinv.at[0:8], dinv.at[0:8], inv_send, inv_recv.at[0], mate).wait_send()
     copy(tx, tx, x_send, x_recv.at[0], mate).wait_send()
 
@@ -417,18 +446,20 @@
 def amplitude_block(integrals, slots, factor, occ, slab, virt):
     dma = pltpu.SemaphoreType.DMA
     vmem = pl.BlockSpec(memory_space=pltpu.VMEM)
-    smem = pl.BlockSpec(memory_space=pltpu.SMEM)
+    hbm = pl.BlockSpec(memory_space=pltpu.HBM)
     return pl.pallas_call(
         fused_kernel,
         out_shape=jax.ShapeDtypeStruct((192, 1536), F32),
-        in_specs=[vmem, vmem, pl.BlockSpec(memory_space=pl.ANY), smem, smem, vmem],
+        in_specs=[vmem, vmem, hbm, pl.BlockSpec(memory_space=pltpu.SMEM), hbm, vmem],
         out_specs=vmem,
         scratch_shapes=[
+            pltpu.SMEM((1,), jnp.int32),
             pltpu.VMEM((8, 34, 2, 32, 256), F32),
             pltpu.VMEM((8, 2, 2, 2, 32, 256), F32),
             pltpu.VMEM((16, 128, 128), F32),
             pltpu.VMEM((4, 128, 128), F32),
             pltpu.VMEM((16, 256, 256), F32),
+            pltpu.VMEM((64, 32, 96), F32),
             pltpu.VMEM((64, 32, 96), F32),
             pltpu.VMEM((64, 32, 96), F32),
             pltpu.VMEM((16, 2, 2, 64, 96), F32),
@@ -447,13 +478,13 @@
             pltpu.VMEM((4, 192, 384), F32),
             pltpu.VMEM((4, 192, 384), F32),
             pltpu.VMEM((2, 96, 384), F32),
-            dma((16,)), dma((16,)), dma((16,)), dma((2,)), dma((2, 4)), dma, dma, dma, dma((4,)),
+            dma, dma((16,)), dma((16,)), dma((16,)), dma((2,)), dma((2, 4)), dma, dma((16,)), dma, dma((4,)),
             dma((16,)), dma((16,)), dma, dma((16,)),
             dma((3, 16)), dma((3, 16)), dma((3, 16)), dma((3, 16)), dma((16,)), dma((16,)),
             dma((4,)), dma((4,)), dma((6,)), dma((6,)),
         ],
         compiler_params=pltpu.CompilerParams(
-            collective_id=0, has_side_effects=True, vmem_limit_bytes=60 * 2**20),
+            collective_id=0, has_side_effects=True, vmem_limit_bytes=52 * 2**20),
     )(integrals, slots, factor, occ, slab, virt)
 
 

time: 137 us -> 134 us (0.978)
  Pallas kernels: 133 us -> 128 us
  local copies, waits for them, and re-layouts: 2.36 us -> 4.17 us
    pallas_call x1, Pallas kernels: 133 us -> 128 us  [amplitude_block(): pl.pallas_call(fused_kernel, out_shape=jax.ShapeDtypeStruct((192, 1536),...]
    unnamed x1 -> x9, local copies, waits for them, and re-layouts: 2.36 us -> 4.17 us
where the time goes in v5:
time: 134 us; the launch traced here: 133 us
  Pallas kernels  128 us (96%)
  local copies, waits for them, and re-layouts  4.17 us (3%)
    pallas_call x1, Pallas kernels, amplitude_block(): pl.pallas_call(fused_kernel, out_shape=jax.ShapeDtypeStruct((192, 1536),...  128 us
    unnamed x9, local copies, waits for them, and re-layouts  4.17 us

profile of v5, /device:TPU:5, one launch (start us, length us, event | category | flops | bytes accessed | tf_op | source)
XLA Modules:
  0.0 133.1 jit_solution(12243587700427971013)
XLA Ops:
  0.7 0.0 copy-start
  0.7 1.1 copy-done
  1.8 0.0 copy-start.1
  1.8 0.7 copy-done.1
  2.5 0.0 copy-start.2
  2.5 0.7 copy-done.2
  3.2 0.0 copy-start.3
  3.2 0.7 copy-done.3
  3.8 128.2 %shard_map.64 = f32[192,1536]{1,0:T(8,128)S(1)} custom-call(f32[32,6144]{1,0:T(8,128)S(1)} %bitcast.4, s32[1,32]{1,0:T(1,128)S(1)} %bitcast.6, f32[32,32,4096]{2,1,0:T(8,128)} %bitcast.7, f32[384]{0:T(512)S(1)} %copy-done.2, s32[1]{0:T(128)S(6)} %copy.8.slab_hbm, f32[1,2048]{1,0:T(1,128)S(1)} %bitcast.5), custom_call_target="tpu_custom_call" | custom-call | tf_op jit(solution)/shard_map/pallas_call | solution.py:450
  132.0 1.0 copy.9
Async XLA Ops:
  0.7 1.1 copy-start
  1.8 0.7 copy-start.1
  2.5 0.7 copy-start.2
  3.2 0.7 copy-start.3

commit v6 on v5

--- a/solution.py
+++ b/solution.py
@@ -39,10 +39,10 @@
     return jnp.where(i < 8, i, 15 - i), jnp.where(i < 8, r - 2 * i, r + 2)
 
 
-def fused_kernel(integrals, slots, factor, occ, slab_hbm, virt, out, slab, pan, blocks, half_inv, half_tmp, dinv, sb, rhs, known, gbuf,
+def fused_kernel(integrals, slots, factor, occ, slab_hbm, virt, out, slab, pan, blocks, half_inv, half_tmp, dinv, sb, rhs, known, near, both, gbuf,
                  xh, xlow, xbuf, tx, rowbuf, colbuf, acc, cols, colh, coll, pairs, exch, total, final, relay,
                  in_local, pan_local, pan_send, pan_recv, diag_send, diag_recv, a_send, a_recv,
-                 inv_send, inv_recv, g_send, g_recv, x_send, x_recv,
+                 inv_send, inv_recv, n_send, n_recv, m_send, m_recv, g_send, g_recv, x_send, x_recv,
                  y_send, y_recv, z_send, z_recv, s_send, s_recv, t_send, t_recv, e_send, e_recv):
     blk, sub = lax.axis_index("blk"), lax.axis_index("sub")
     hi = blk // 16
@@ -117,6 +117,10 @@
             copy(slab_of(2 * j + 1 - core, q), slab_place(j, q, core), diag_send.at[q], diag_recv.at[q, j // 2],
                  mate).start()
 
+    for p in range(8):
+        copy(factor.at[4 * p + 2:4 * p + 4, :, 512 * p:512 * p + 256], near.at[p, :, core],
+             n_send, n_recv, beside(1 if p < 4 else -1, core)).start()
+
     def spread(k, _):
         to = (blk + k) % 32
         for c in range(2):
@@ -132,8 +136,8 @@
         k, row = panel_place(i, 2 * i)
         piece = factor.at[2 * i:32, :, 256 * i:256 * i + 256]
         place = pan.at[k, row:row + 32 - 2 * i, core]
-        pltpu.make_async_copy(piece, place, pan_local.at[i]).start()
-        copy(piece, place, pan_send.at[i], pan_recv.at[i], mate).start()
+        pltpu.make_async_copy(piece, place, pan_local).start()
+        copy(piece, place, pan_send, pan_recv, mate).start()
 
     pltpu.make_async_copy(slab_hbm, slab, in_local).wait()
     for t in range(3):
@@ -187,7 +191,7 @@
 
     def offer(i, value):
         gbuf[i, :, xl] = value.reshape(2, 64, 96)
-        copy(gbuf.at[i, :, xl], gbuf.at[i, :, xl], g_send.at[i], g_recv.at[i], peer).start()
+        copy(gbuf.at[i, :, xl], gbuf.at[i, :, xl], g_send, g_recv.at[i], peer).start()
 
     def right_side(i):
         for count, here in ((3, blk // 2 == i), (4, blk // 2 != i)):
@@ -198,42 +202,49 @@
 
         return rhs[pl.ds(4 * i, 4)].reshape(128, 96)
 
-    def factor_part(i, t):
+    def factor_rows(i, t, count):
         k, at = panel_place(i, 2 * t)
-        return split(pan[k, pl.ds(at, 2)].reshape(128, 256))
+        return split(pan[k, pl.ds(at, 2 * count)].reshape(128 * count, 256))
+
+    def times_solved(part, which):
+        return dot3(part, (xh[which], xlow[which]), NN)
+
+    def learn(u, i, which):
+        rows = pl.ds(8 * u, 8)
+        known[rows] = known[rows] + times_solved(factor_rows(i, 2 * u, 2), which).reshape(8, 32, 96)
 
     def own_out(i):
         half = rowbuf.at[y, i, 1 - core]
         copy(half, half, x_send, x_recv.at[i], mate).wait_recv()
         for k, offset in enumerate((1, -1)):
-            copy(rowbuf.at[y, i], rowbuf.at[y, i], y_send.at[k, i], y_recv.at[k, i], y_at(offset)).start()
+            copy(rowbuf.at[y, i], rowbuf.at[y, i], y_send, y_recv.at[k, i], y_at(offset)).start()
 
         @pl.when(same)
         def _():
             for k, offset in enumerate((1, -1)):
-                copy(rowbuf.at[y, i], colbuf.at[z, i], z_send.at[k, i], z_recv.at[k, i], z_at(offset)).start()
+                copy(rowbuf.at[y, i], colbuf.at[z, i], z_send, z_recv.at[k, i], z_at(offset)).start()
             colbuf[z, i] = rowbuf[y, i]
 
         @pl.when(jnp.logical_not(same))
         def _():
-            copy(rowbuf.at[y, i], colbuf.at[z, i], s_send.at[i], s_recv.at[i], swap).start()
+            copy(rowbuf.at[y, i], colbuf.at[z, i], s_send, s_recv.at[i], swap).start()
 
     def swapped_out(i):
         @pl.when(jnp.logical_not(same))
         def _():
-            copy(colbuf.at[z, i], colbuf.at[z, i], s_send.at[i], s_recv.at[i], swap).wait_recv()
+            copy(colbuf.at[z, i], colbuf.at[z, i], s_send, s_recv.at[i], swap).wait_recv()
             for k, offset in enumerate((1, -1)):
-                copy(colbuf.at[z, i], colbuf.at[z, i], z_send.at[k, i], z_recv.at[k, i], z_at(offset)).start()
+                copy(colbuf.at[z, i], colbuf.at[z, i], z_send, z_recv.at[k, i], z_at(offset)).start()
 
     def got(buf, send, recv, place, k, i):
-        copy(buf.at[place, i], buf.at[place, i], send.at[k, i], recv.at[k, i], mate).wait_recv()
+        copy(buf.at[place, i], buf.at[place, i], send, recv.at[k, i], mate).wait_recv()
 
     def forward(buf, send, recv, me, at, i):
         odd = i % 2
         step = 1 - 2 * odd
         src = (me - step + 4) % 4
         got(buf, send, recv, src, odd, i)
-        copy(buf.at[src, i], buf.at[src, i], send.at[2, i], recv.at[2, i], at(step)).start()
+        copy(buf.at[src, i], buf.at[src, i], send, recv.at[2, i], at(step)).start()
 
     def forward_y(i):
         forward(rowbuf, y_send, y_recv, y, y_at, i)
@@ -270,89 +281,112 @@
         lax.fori_loop(2 * half, 2 * half + 2, part, 0)
 
     acc[...] = jnp.zeros_like(acc)
-    for i in range(16):
-        k, row = panel_place(i, 2 * i)
-        piece = pan.at[k, row:row + 32 - 2 * i, core]
-        pltpu.make_async_copy(piece, piece, pan_local.at[i]).wait()
-        copy(piece, piece, pan_send.at[i], pan_recv.at[i], mate).wait_recv()
+    piece = pan.at[:, :, core]
+    pltpu.make_async_copy(piece, piece, pan_local).wait()
+    copy(piece, piece, pan_send, pan_recv, mate).wait_recv()
+    piece = near.at[:, :, core]
+    copy(piece, piece, n_send, n_recv, mate).wait_recv()
+    copy(piece, piece, m_send, m_recv, mate).start()
     known[...] = jnp.zeros_like(known)
     offer(0, right_side(0))
-
-    def round_of(i, _):
-        @pl.when(i % 4 == 0)
-        def _():
-            copy(dinv.at[0:2], dinv.at[0:2], inv_send, inv_recv.at[i // 4], mate).wait_recv()
-
-        inverse = split(dinv[i])
-
-        @pl.when(i > 0)
-        def _():
+    offer(1, right_side(1))
+
+    def incoming(i):
+        other = gbuf.at[i, :, 1 - xl]
+        copy(other, other, g_send, g_recv.at[i], peer).wait_recv()
+
+    def solved_round(i, which, value):
+        solved = dot3(split(dinv[i]), split(value.reshape(256, 96)), NN)
+        high, low = split(solved)
+        xh[which] = high
+        xlow[which] = low
+        xbuf[which] = solved.reshape(2, 128, 96)
+
+    def spread_round(i, which):
+        tx[i] = xbuf[which, 1 - core].T
+        copy(tx.at[i], rowbuf.at[y, i, core], x_send, x_recv.at[i], mate).start()
+        rowbuf[y, i, core] = xbuf[which, core].T
+
+    def pair_of(p, _):
+        a = 2 * p
+        b = a + 1
+
+        @pl.when(p % 2 == 0)
+        def _():
+            copy(dinv.at[0:2], dinv.at[0:2], inv_send, inv_recv.at[p // 2], mate).wait_recv()
+
+        @pl.when(p == 0)
+        def _():
+            other = near.at[:, :, 1 - core]
+            copy(other, other, m_send, m_recv, mate).wait_recv()
+
+        @pl.when(p > 0)
+        def _():
+            own_out(a - 1)
+
             def later(u, _):
-                k, at = panel_place(i - 1, 4 * u)
-                part = split(pan[k, pl.ds(at, 4)].reshape(256, 256))
-                term = dot3(part, (xh[...], xlow[...]), NN)
-                rows = pl.ds(8 * u, 8)
-                known[rows] = known[rows] + term.reshape(8, 32, 96)
+                learn(u, a - 2, 0)
+                learn(u, a - 1, 1)
                 return 0
 
-            lax.fori_loop((i + 1) // 2, 8, later, 0)
-            own_out(i - 1)
-
-        @pl.when(i > 1)
-        def _():
-            swapped_out(i - 2)
-
-        @pl.when((i > 5) & (i % 2 == 0))
-        def _():
-            arrived((i - 6) // 2)
-
-        @pl.when(i > 5)
-        def _():
-            product_half((i - 6) // 2, i % 2)
-
-        @pl.when(i > 1)
-        def _():
-            forward_y(i - 2)
-
-        @pl.when(i > 2)
-        def _():
-            forward_z(i - 3)
-
-        @pl.when(i < 15)
-        def _():
-            rest = right_side(i + 1) - known[pl.ds(4 * i + 4, 4)].reshape(128, 96)
-            rhs[pl.ds(4 * i + 4, 4)] = rest.reshape(4, 32, 96)
-
-        other = gbuf.at[i, :, 1 - xl]
-        copy(other, other, g_send.at[i], g_recv.at[i], peer).wait_recv()
-        solved = dot3(inverse, split(gbuf[i].reshape(256, 96)), NN)
-        high, low = split(solved)
-        xh[...] = high
-        xlow[...] = low
-
-        @pl.when(i < 15)
-        def _():
-            term = dot3(factor_part(i, i + 1), (high, low), NN)
-            offer(i + 1, rhs[pl.ds(4 * i + 4, 4)].reshape(128, 96) - term)
-
-        xbuf[...] = solved.reshape(2, 128, 96)
-        tx[i] = xbuf[1 - core].T
-        copy(tx.at[i], rowbuf.at[y, i, core], x_send, x_recv.at[i], mate).start()
-        rowbuf[y, i, core] = xbuf[core].T
+            lax.fori_loop(p + 1, 8, later, 0)
+
+        @pl.when(p > 2)
+        def _():
+            arrived(p - 3)
+            product_half(p - 3, 0)
+            product_half(p - 3, 1)
+
+        @pl.when(p > 0)
+        def _():
+            forward_y(a - 2)
+
+        @pl.when(p > 1)
+        def _():
+            forward_z(a - 4)
+            forward_z(a - 3)
+
+        incoming(a)
+        solved_round(a, 0, gbuf[a])
+        both[:, xl] = gbuf[b, :, xl] - times_solved(factor_rows(a, b, 1), 0).reshape(2, 64, 96)
+        far = times_solved(split(near[p].reshape(128, 256)), 0).reshape(2, 64, 96)
+        spread_round(a, 0)
+        incoming(b)
+        both[:, 1 - xl] = gbuf[b, :, 1 - xl] - far
+        solved_round(b, 1, both[...])
+
+        @pl.when(p < 7)
+        def _():
+            learn(p + 1, a, 0)
+            for c in range(2):
+                term = times_solved(factor_rows(b, a + 2 + c, 1), 1)
+                rows = pl.ds(4 * (a + 2 + c), 4)
+                offer(a + 2 + c, right_side(a + 2 + c) - known[rows].reshape(128, 96) - term)
+
+        spread_round(b, 1)
+        own_out(a)
+
+        @pl.when(p > 0)
+        def _():
+            swapped_out(a - 2)
+            swapped_out(a - 1)
+            forward_y(a - 1)
+
         return 0
 
-    lax.fori_loop(0, 16, round_of, 0)
+    lax.fori_loop(0, 8, pair_of, 0)
 
     own_out(15)
+    forward_z(12)
+    forward_z(13)
     swapped_out(14)
     forward_y(14)
-    forward_z(13)
-    swapped_out(15)
     arrived(5)
     product_half(5, 0)
-    forward_z(14)
+    swapped_out(15)
     forward_y(15)
     product_half(5, 1)
+    forward_z(14)
     arrived(6)
     product_half(6, 0)
     forward_z(15)
@@ -415,26 +449,21 @@
     for n in range(4):
         trade(n).wait_send()
 
-    def drain(i, _):
-        piece = rowbuf.at[y, i]
-        for k in range(3):
-            copy(piece, piece, y_send.at[k, i], y_recv.at[k, i], mate).wait_send()
-            copy(piece, piece, z_send.at[k, i], z_recv.at[k, i], mate).wait_send()
-
-        @pl.when(jnp.logical_not(same))
-        def _():
-            copy(piece, piece, s_send.at[i], s_recv.at[i], swap).wait_send()
-
-        return 0
-
-    lax.fori_loop(0, 16, drain, 0)
-
-    for i in range(16):
-        k, row = panel_place(i, 2 * i)
-        piece = pan.at[k, row:row + 32 - 2 * i, core]
-        copy(piece, piece, pan_send.at[i], pan_recv.at[i], mate).wait_send()
-        mine = gbuf.at[i, :, xl]
-        copy(mine, mine, g_send.at[i], g_recv.at[i], peer).wait_send()
+    piece = rowbuf.at[0:3]
+    copy(piece, piece, y_send, y_recv.at[0, 0], mate).wait_send()
+    copy(piece, piece, z_send, z_recv.at[0, 0], mate).wait_send()
+
+    @pl.when(jnp.logical_not(same))
+    def _():
+        copy(rowbuf.at[0], rowbuf.at[0], s_send, s_recv.at[0], swap).wait_send()
+
+    piece = pan.at[:, :, core]
+    copy(piece, piece, pan_send, pan_recv, mate).wait_send()
+    piece = gbuf.at[:, :, xl]
+    copy(piece, piece, g_send, g_recv.at[0], peer).wait_send()
+    piece = near.at[:, :, core]
+    copy(piece, piece, n_send, n_recv, mate).wait_send()
+    copy(piece, piece, m_send, m_recv, mate).wait_send()
     for q in range(2):
         piece = blocks.at[0:6, q, :, :, :, 0:128 * (q + 1)]
         copy(piece, piece, diag_send.at[q], diag_recv.at[q, 0], mate).wait_send()
@@ -462,10 +491,12 @@
             pltpu.VMEM((64, 32, 96), F32),
             pltpu.VMEM((64, 32, 96), F32),
             pltpu.VMEM((64, 32, 96), F32),
+            pltpu.VMEM((8, 2, 2, 32, 256), F32),
+            pltpu.VMEM((2, 2, 64, 96), F32),
             pltpu.VMEM((16, 2, 2, 64, 96), F32),
-            pltpu.VMEM((256, 96), BF16),
-            pltpu.VMEM((256, 96), BF16),
-            pltpu.VMEM((2, 128, 96), F32),
+            pltpu.VMEM((2, 256, 96), BF16),
+            pltpu.VMEM((2, 256, 96), BF16),
+            pltpu.VMEM((2, 2, 128, 96), F32),
             pltpu.VMEM((16, 96, 128), F32),
             pltpu.VMEM((4, 16, 2, 96, 128), F32),
             pltpu.VMEM((4, 16, 2, 96, 128), F32),
@@ -478,9 +509,9 @@
             pltpu.VMEM((4, 192, 384), F32),
             pltpu.VMEM((4, 192, 384), F32),
             pltpu.VMEM((2, 96, 384), F32),
-            dma, dma((16,)), dma((16,)), dma((16,)), dma((2,)), dma((2, 4)), dma, dma((16,)), dma, dma((4,)),
-            dma((16,)), dma((16,)), dma, dma((16,)),
-            dma((3, 16)), dma((3, 16)), dma((3, 16)), dma((3, 16)), dma((16,)), dma((16,)),
+            dma, dma, dma, dma, dma((2,)), dma((2, 4)), dma, dma((16,)), dma, dma((4,)),
+            dma, dma, dma, dma, dma, dma((16,)), dma, dma((16,)),
+            dma, dma((3, 16)), dma, dma((3, 16)), dma, dma((16,)),
             dma((4,)), dma((4,)), dma((6,)), dma((6,)),
         ],
         compiler_params=pltpu.CompilerParams(

time: 134 us -> 143 us (1.067)
  Pallas kernels: 128 us -> 137 us
    pallas_call x1, Pallas kernels: 128 us -> 137 us  [amplitude_block(): pl.pallas_call(fused_kernel, out_shape=jax.ShapeDtypeStruct((192, 1536),...]
where the time goes in v6:
time: 143 us; the launch traced here: 142 us
  Pallas kernels  137 us (96%)
  local copies, waits for them, and re-layouts  4.17 us (3%)
    pallas_call x1, Pallas kernels, amplitude_block(): pl.pallas_call(fused_kernel, out_shape=jax.ShapeDtypeStruct((192, 1536),...  137 us
    unnamed x9, local copies, waits for them, and re-layouts  4.17 us

profile of v6, /device:TPU:5, one launch (start us, length us, event | category | flops | bytes accessed | tf_op | source)
XLA Modules:
  0.0 142.2 jit_solution(10246392871129326127)
XLA Ops:
  0.7 0.0 copy-start
  0.7 1.1 copy-done
  1.8 0.0 copy-start.1
  1.8 0.7 copy-done.1
  2.5 0.0 copy-start.2
  2.5 0.7 copy-done.2
  3.2 0.0 copy-start.3
  3.2 0.7 copy-done.3
  3.8 137.3 %shard_map.64 = f32[192,1536]{1,0:T(8,128)S(1)} custom-call(f32[32,6144]{1,0:T(8,128)S(1)} %bitcast.4, s32[1,32]{1,0:T(1,128)S(1)} %bitcast.6, f32[32,32,4096]{2,1,0:T(8,128)} %bitcast.7, f32[384]{0:T(512)S(1)} %copy-done.2, s32[1]{0:T(128)S(6)} %copy.8.slab_hbm, f32[1,2048]{1,0:T(1,128)S(1)} %bitcast.5), custom_call_target="tpu_custom_call" | custom-call | tf_op jit(solution)/shard_map/pallas_call | solution.py:479
  141.2 1.0 copy.9
Async XLA Ops:
  0.7 1.1 copy-start
  1.8 0.7 copy-start.1
  2.5 0.7 copy-start.2
  3.2 0.7 copy-start.3

commit v7 on v5

--- a/solution.py
+++ b/solution.py
@@ -41,7 +41,7 @@
 
 def fused_kernel(integrals, slots, factor, occ, slab_hbm, virt, out, slab, pan, blocks, half_inv, half_tmp, dinv, sb, rhs, known, gbuf,
                  xh, xlow, xbuf, tx, rowbuf, colbuf, acc, cols, colh, coll, pairs, exch, total, final, relay,
-                 in_local, pan_local, pan_send, pan_recv, diag_send, diag_recv, a_send, a_recv,
+                 in_local, pan_send, pan_recv, diag_send, diag_recv, a_send, a_recv,
                  inv_send, inv_recv, g_send, g_recv, x_send, x_recv,
                  y_send, y_recv, z_send, z_recv, s_send, s_recv, t_send, t_recv, e_send, e_recv):
     blk, sub = lax.axis_index("blk"), lax.axis_index("sub")
@@ -117,6 +117,17 @@
             copy(slab_of(2 * j + 1 - core, q), slab_place(j, q, core), diag_send.at[q], diag_recv.at[q, j // 2],
                  mate).start()
 
+    def panels(first, last):
+        for i in range(first, last):
+            k, row = panel_place(i, 2 * i + 2)
+            piece = factor.at[2 * i + 2:32, :, 256 * i:256 * i + 256]
+            place = pan.at[k, row:row + 30 - 2 * i, core]
+            group = (i > 1) + (i > 3) + (i > 7)
+            pltpu.make_async_copy(piece, place, pan_recv.at[group]).start()
+            copy(piece, place, pan_send, pan_recv.at[group], mate).start()
+
+    panels(0, 4)
+
     def spread(k, _):
         to = (blk + k) % 32
         for c in range(2):
@@ -128,12 +139,7 @@
     copy(sb.at[2 * blk + 1 - core], rhs.at[2 * blk + core], a_send, a_recv.at[blk // 2], mate).start()
     rhs[2 * blk + core] = sb[2 * blk + core]
 
-    for i in range(16):
-        k, row = panel_place(i, 2 * i)
-        piece = factor.at[2 * i:32, :, 256 * i:256 * i + 256]
-        place = pan.at[k, row:row + 32 - 2 * i, core]
-        pltpu.make_async_copy(piece, place, pan_local.at[i]).start()
-        copy(piece, place, pan_send.at[i], pan_recv.at[i], mate).start()
+    panels(4, 15)
 
     pltpu.make_async_copy(slab_hbm, slab, in_local).wait()
     for t in range(3):
@@ -187,7 +193,7 @@
 
     def offer(i, value):
         gbuf[i, :, xl] = value.reshape(2, 64, 96)
-        copy(gbuf.at[i, :, xl], gbuf.at[i, :, xl], g_send.at[i], g_recv.at[i], peer).start()
+        copy(gbuf.at[i, :, xl], gbuf.at[i, :, xl], g_send, g_recv.at[i], peer).start()
 
     def right_side(i):
         for count, here in ((3, blk // 2 == i), (4, blk // 2 != i)):
@@ -206,34 +212,34 @@
         half = rowbuf.at[y, i, 1 - core]
         copy(half, half, x_send, x_recv.at[i], mate).wait_recv()
         for k, offset in enumerate((1, -1)):
-            copy(rowbuf.at[y, i], rowbuf.at[y, i], y_send.at[k, i], y_recv.at[k, i], y_at(offset)).start()
+            copy(rowbuf.at[y, i], rowbuf.at[y, i], y_send, y_recv.at[k, i], y_at(offset)).start()
 
         @pl.when(same)
         def _():
             for k, offset in enumerate((1, -1)):
-                copy(rowbuf.at[y, i], colbuf.at[z, i], z_send.at[k, i], z_recv.at[k, i], z_at(offset)).start()
+                copy(rowbuf.at[y, i], colbuf.at[z, i], z_send, z_recv.at[k, i], z_at(offset)).start()
             colbuf[z, i] = rowbuf[y, i]
 
         @pl.when(jnp.logical_not(same))
         def _():
-            copy(rowbuf.at[y, i], colbuf.at[z, i], s_send.at[i], s_recv.at[i], swap).start()
+            copy(rowbuf.at[y, i], colbuf.at[z, i], s_send, s_recv.at[i], swap).start()
 
     def swapped_out(i):
         @pl.when(jnp.logical_not(same))
         def _():
-            copy(colbuf.at[z, i], colbuf.at[z, i], s_send.at[i], s_recv.at[i], swap).wait_recv()
+            copy(colbuf.at[z, i], colbuf.at[z, i], s_send, s_recv.at[i], swap).wait_recv()
             for k, offset in enumerate((1, -1)):
-                copy(colbuf.at[z, i], colbuf.at[z, i], z_send.at[k, i], z_recv.at[k, i], z_at(offset)).start()
+                copy(colbuf.at[z, i], colbuf.at[z, i], z_send, z_recv.at[k, i], z_at(offset)).start()
 
     def got(buf, send, recv, place, k, i):
-        copy(buf.at[place, i], buf.at[place, i], send.at[k, i], recv.at[k, i], mate).wait_recv()
+        copy(buf.at[place, i], buf.at[place, i], send, recv.at[k, i], mate).wait_recv()
 
     def forward(buf, send, recv, me, at, i):
         odd = i % 2
         step = 1 - 2 * odd
         src = (me - step + 4) % 4
         got(buf, send, recv, src, odd, i)
-        copy(buf.at[src, i], buf.at[src, i], send.at[2, i], recv.at[2, i], at(step)).start()
+        copy(buf.at[src, i], buf.at[src, i], send, recv.at[2, i], at(step)).start()
 
     def forward_y(i):
         forward(rowbuf, y_send, y_recv, y, y_at, i)
@@ -270,15 +276,16 @@
         lax.fori_loop(2 * half, 2 * half + 2, part, 0)
 
     acc[...] = jnp.zeros_like(acc)
-    for i in range(16):
-        k, row = panel_place(i, 2 * i)
-        piece = pan.at[k, row:row + 32 - 2 * i, core]
-        pltpu.make_async_copy(piece, piece, pan_local.at[i]).wait()
-        copy(piece, piece, pan_send.at[i], pan_recv.at[i], mate).wait_recv()
     known[...] = jnp.zeros_like(known)
     offer(0, right_side(0))
 
     def round_of(i, _):
+        for group, (at, many, wide) in enumerate(((0, 2, 29), (2, 2, 25), (4, 4, 19), (8, 4, 14))):
+            @pl.when(i == at)
+            def _(group=group, many=many, wide=wide):
+                piece = pan.at[0:many, 0:wide]
+                pltpu.make_async_copy(piece, piece, pan_recv.at[group]).wait()
+
         @pl.when(i % 4 == 0)
         def _():
             copy(dinv.at[0:2], dinv.at[0:2], inv_send, inv_recv.at[i // 4], mate).wait_recv()
@@ -324,7 +331,7 @@
             rhs[pl.ds(4 * i + 4, 4)] = rest.reshape(4, 32, 96)
 
         other = gbuf.at[i, :, 1 - xl]
-        copy(other, other, g_send.at[i], g_recv.at[i], peer).wait_recv()
+        copy(other, other, g_send, g_recv.at[i], peer).wait_recv()
         solved = dot3(inverse, split(gbuf[i].reshape(256, 96)), NN)
         high, low = split(solved)
         xh[...] = high
@@ -415,26 +422,18 @@
     for n in range(4):
         trade(n).wait_send()
 
-    def drain(i, _):
-        piece = rowbuf.at[y, i]
-        for k in range(3):
-            copy(piece, piece, y_send.at[k, i], y_recv.at[k, i], mate).wait_send()
-            copy(piece, piece, z_send.at[k, i], z_recv.at[k, i], mate).wait_send()
-
-        @pl.when(jnp.logical_not(same))
-        def _():
-            copy(piece, piece, s_send.at[i], s_recv.at[i], swap).wait_send()
-
-        return 0
-
-    lax.fori_loop(0, 16, drain, 0)
-
-    for i in range(16):
-        k, row = panel_place(i, 2 * i)
-        piece = pan.at[k, row:row + 32 - 2 * i, core]
-        copy(piece, piece, pan_send.at[i], pan_recv.at[i], mate).wait_send()
-        mine = gbuf.at[i, :, xl]
-        copy(mine, mine, g_send.at[i], g_recv.at[i], peer).wait_send()
+    piece = rowbuf.at[0:3]
+    copy(piece, piece, y_send, y_recv.at[0, 0], mate).wait_send()
+    copy(piece, piece, z_send, z_recv.at[0, 0], mate).wait_send()
+
+    @pl.when(jnp.logical_not(same))
+    def _():
+        copy(rowbuf.at[0], rowbuf.at[0], s_send, s_recv.at[0], swap).wait_send()
+
+    piece = pan.at[:, 0:30, core]
+    copy(piece, piece, pan_send, pan_recv.at[0], mate).wait_send()
+    piece = gbuf.at[:, :, xl]
+    copy(piece, piece, g_send, g_recv.at[0], peer).wait_send()
     for q in range(2):
         piece = blocks.at[0:6, q, :, :, :, 0:128 * (q + 1)]
         copy(piece, piece, diag_send.at[q], diag_recv.at[q, 0], mate).wait_send()
@@ -478,9 +477,9 @@
             pltpu.VMEM((4, 192, 384), F32),
             pltpu.VMEM((4, 192, 384), F32),
             pltpu.VMEM((2, 96, 384), F32),
-            dma, dma((16,)), dma((16,)), dma((16,)), dma((2,)), dma((2, 4)), dma, dma((16,)), dma, dma((4,)),
-            dma((16,)), dma((16,)), dma, dma((16,)),
-            dma((3, 16)), dma((3, 16)), dma((3, 16)), dma((3, 16)), dma((16,)), dma((16,)),
+            dma, dma, dma((4,)), dma((2,)), dma((2, 4)), dma, dma((16,)), dma, dma((4,)),
+            dma, dma((16,)), dma, dma((16,)),
+            dma, dma((3, 16)), dma, dma((3, 16)), dma, dma((16,)),
             dma((4,)), dma((4,)), dma((6,)), dma((6,)),
         ],
         compiler_params=pltpu.CompilerParams(

time: 134 us -> 133 us (level)
  Pallas kernels: 128 us -> 126 us
    pallas_call x1, Pallas kernels: 128 us -> 126 us  [amplitude_block(): pl.pallas_call(fused_kernel, out_shape=jax.ShapeDtypeStruct((192, 1536),...]
where the time goes in v7:
time: 133 us; the launch traced here: 131 us
  Pallas kernels  126 us (95%)
  local copies, waits for them, and re-layouts  4.17 us (3%)
    pallas_call x1, Pallas kernels, amplitude_block(): pl.pallas_call(fused_kernel, out_shape=jax.ShapeDtypeStruct((192, 1536),...  126 us
    unnamed x9, local copies, waits for them, and re-layouts  4.17 us

profile of v7, /device:TPU:5, one launch (start us, length us, event | category | flops | bytes accessed | tf_op | source)
XLA Modules:
  0.0 131.3 jit_solution(11311387461176856470)
XLA Ops:
  0.7 0.0 copy-start
  0.7 1.1 copy-done
  1.8 0.0 copy-start.1
  1.8 0.7 copy-done.1
  2.5 0.0 copy-start.2
  2.5 0.7 copy-done.2
  3.2 0.0 copy-start.3
  3.2 0.7 copy-done.3
  3.8 126.5 %shard_map.64 = f32[192,1536]{1,0:T(8,128)S(1)} custom-call(f32[32,6144]{1,0:T(8,128)S(1)} %bitcast.4, s32[1,32]{1,0:T(1,128)S(1)} %bitcast.6, f32[32,32,4096]{2,1,0:T(8,128)} %bitcast.7, f32[384]{0:T(512)S(1)} %copy-done.2, s32[1]{0:T(128)S(6)} %copy.8.slab_hbm, f32[1,2048]{1,0:T(1,128)S(1)} %bitcast.5), custom_call_target="tpu_custom_call" | custom-call | tf_op jit(solution)/shard_map/pallas_call | solution.py:449
  130.3 1.0 copy.9
Async XLA Ops:
  0.7 1.1 copy-start
  1.8 0.7 copy-start.1
  2.5 0.7 copy-start.2
  3.2 0.7 copy-start.3

commit v8 on v7

--- a/solution.py
+++ b/solution.py
@@ -105,7 +105,8 @@
         low = (rest - mid.astype(F32)).astype(BF16)
         picked = pick(high) + (pick(mid) + pick(low))
         for k in range(4):
-            sb[4 * g + k] = picked[:, 96 * k:96 * k + 96]
+            sb[4 * g + k] = jnp.concatenate(
+                [picked[8 * m:8 * m + 8, 96 * k:96 * k + 96] for m in range(4)], axis=1)
 
     pl.semaphore_wait(barrier, 67)
 
@@ -128,14 +129,24 @@
 
     panels(0, 4)
 
-    def spread(k, _):
-        to = (blk + k) % 32
+    def send_right_side(to):
         for c in range(2):
             copy(sb.at[2 * to + c], rhs.at[2 * blk + core], a_send, a_recv.at[blk // 2],
                  {"blk": to, "sub": 2 * xl + c}).start()
+
+    def cross(k, _):
+        send_right_side((1 - hi) * 16 + (blk + k) % 16)
         return 0
 
-    lax.fori_loop(1, 32, spread, 0)
+    def spread(k, _):
+        send_right_side(hi * 16 + (blk + k) % 16)
+        return 0
+
+    @pl.when(hi == 0)
+    def _():
+        lax.fori_loop(0, 16, cross, 0)
+
+    lax.fori_loop(1, 16, spread, 0)
     copy(sb.at[2 * blk + 1 - core], rhs.at[2 * blk + core], a_send, a_recv.at[blk // 2], mate).start()
     rhs[2 * blk + core] = sb[2 * blk + core]
 
@@ -153,6 +164,10 @@
         for q in range(2):
             piece = blocks.at[pl.ds(2 * g, 2), q, :, :, :, 0:128 * (q + 1)]
             pltpu.make_async_copy(piece, piece, diag_recv.at[q, g]).wait()
+
+        @pl.when((turn == 2) & (hi == 1))
+        def _():
+            lax.fori_loop(0, 16, cross, 0)
 
         def block(n):
             q = n % 2
@@ -202,7 +217,8 @@
                 piece = rhs.at[0:count]
                 copy(piece, piece, a_send, a_recv.at[i], mate).wait_recv()
 
-        return rhs[pl.ds(4 * i, 4)].reshape(128, 96)
+        packed = rhs[pl.ds(4 * i, 4)]
+        return jnp.concatenate([packed[:, :, 96 * m:96 * m + 96] for m in range(4)], axis=1).reshape(128, 96)
 
     def factor_part(i, t):
         k, at = panel_place(i, 2 * t)
@@ -328,7 +344,7 @@
         @pl.when(i < 15)
         def _():
             rest = right_side(i + 1) - known[pl.ds(4 * i + 4, 4)].reshape(128, 96)
-            rhs[pl.ds(4 * i + 4, 4)] = rest.reshape(4, 32, 96)
+            known[pl.ds(4 * i + 4, 4)] = rest.reshape(4, 32, 96)
 
         other = gbuf.at[i, :, 1 - xl]
         copy(other, other, g_send, g_recv.at[i], peer).wait_recv()
@@ -340,7 +356,7 @@
         @pl.when(i < 15)
         def _():
             term = dot3(factor_part(i, i + 1), (high, low), NN)
-            offer(i + 1, rhs[pl.ds(4 * i + 4, 4)].reshape(128, 96) - term)
+            offer(i + 1, known[pl.ds(4 * i + 4, 4)].reshape(128, 96) - term)
 
         xbuf[...] = solved.reshape(2, 128, 96)
         tx[i] = xbuf[1 - core].T
@@ -458,8 +474,8 @@
             pltpu.VMEM((16, 128, 128), F32),
             pltpu.VMEM((4, 128, 128), F32),
             pltpu.VMEM((16, 256, 256), F32),
-            pltpu.VMEM((64, 32, 96), F32),
-            pltpu.VMEM((64, 32, 96), F32),
+            pltpu.VMEM((64, 8, 384), F32),
+            pltpu.VMEM((64, 8, 384), F32),
             pltpu.VMEM((64, 32, 96), F32),
             pltpu.VMEM((16, 2, 2, 64, 96), F32),
             pltpu.VMEM((256, 96), BF16),

time: 133 us -> 128 us (0.962)
  Pallas kernels: 126 us -> 122 us
    pallas_call x1, Pallas kernels: 126 us -> 122 us  [amplitude_block(): pl.pallas_call(fused_kernel, out_shape=jax.ShapeDtypeStruct((192, 1536),...]
where the time goes in v8:
time: 128 us; the launch traced here: 127 us
  Pallas kernels  122 us (95%)
  local copies, waits for them, and re-layouts  4.17 us (3%)
    pallas_call x1, Pallas kernels, amplitude_block(): pl.pallas_call(fused_kernel, out_shape=jax.ShapeDtypeStruct((192, 1536),...  122 us
    unnamed x9, local copies, waits for them, and re-layouts  4.17 us

profile of v8, /device:TPU:5, one launch (start us, length us, event | category | flops | bytes accessed | tf_op | source)
XLA Modules:
  0.0 126.6 jit_solution(12094179922418538998)
XLA Ops:
  0.7 0.0 copy-start
  0.7 1.1 copy-done
  1.8 0.0 copy-start.1
  1.8 0.7 copy-done.1
  2.5 0.0 copy-start.2
  2.5 0.7 copy-done.2
  3.2 0.0 copy-start.3
  3.2 0.7 copy-done.3
  3.8 121.7 %shard_map.64 = f32[192,1536]{1,0:T(8,128)S(1)} custom-call(f32[32,6144]{1,0:T(8,128)S(1)} %bitcast.4, s32[1,32]{1,0:T(1,128)S(1)} %bitcast.6, f32[32,32,4096]{2,1,0:T(8,128)} %bitcast.7, f32[384]{0:T(512)S(1)} %copy-done.2, s32[1]{0:T(128)S(6)} %copy.8.slab_hbm, f32[1,2048]{1,0:T(1,128)S(1)} %bitcast.5), custom_call_target="tpu_custom_call" | custom-call | tf_op jit(solution)/shard_map/pallas_call | solution.py:465
  125.6 1.0 copy.9
Async XLA Ops:
  0.7 1.1 copy-start
  1.8 0.7 copy-start.1
  2.5 0.7 copy-start.2
  3.2 0.7 copy-start.3

commit v9 on v8

--- a/solution.py
+++ b/solution.py
@@ -390,7 +390,7 @@
         k = order[n]
         return copy(acc.at[k, :, theirs], exch.at[k], t_send.at[n], t_recv.at[n], mate)
 
-    for n in range(4):
+    def finish(n):
         product_rows(7, order[n])
         trade(n).start()
 
@@ -399,6 +399,8 @@
         k = order[n]
         total[k] = acc[k, :, mine] + exch[k]
 
+    finish(0)
+    finish(1)
     summed(0)
     hops = []
     for at, offset in enumerate((1, -1)):
@@ -406,6 +408,7 @@
                          e_send.at[at], e_recv.at[at], y_at(offset)))
         hops[-1].start()
     for n, offset in ((1, 1), (2, -1)):
+        finish(n + 1)
         summed(n)
         hops.append(copy(total.at[order[n]], final.at[y], e_send.at[n + 1], e_recv.at[n + 1], y_at(offset)))
         hops[-1].start()
@@ -504,8 +507,11 @@
 
 
 def shards(integrals, slot_order, factor_rows, occ_energy, slab_index, virt_energy):
-    return amplitude_block(integrals[0, 0], slot_order[0], factor_rows[:, 0],
-                           occ_energy, slab_index, virt_energy[None])
+    def stay(value):
+        return pltpu.with_memory_space_constraint(value, pltpu.HBM)
+
+    return amplitude_block(stay(integrals[0, 0]), stay(slot_order[0]), stay(factor_rows[:, 0]),
+                           stay(occ_energy), slab_index, stay(virt_energy[None]))
 
 
 def solution(mesh):

time: 128 us -> 125 us (0.977)
  local copies, waits for them, and re-layouts: 4.17 us -> 1.02 us
    unnamed x9 -> x1, local copies, waits for them, and re-layouts: 4.17 us -> 1.02 us
where the time goes in v9:
time: 125 us; the launch traced here: 124 us
  Pallas kernels  123 us (98%)
    pallas_call x1, Pallas kernels, amplitude_block(): pl.pallas_call(fused_kernel, out_shape=jax.ShapeDtypeStruct((192, 1536),...  123 us

profile of v9, /device:TPU:5, one launch (start us, length us, event | category | flops | bytes accessed | tf_op | source)
XLA Modules:
  0.0 124.4 jit_solution(2548412607004937042)
XLA Ops:
  0.7 122.8 %shard_map.64 = f32[192,1536]{1,0:T(8,128)S(1)} custom-call(f32[32,6144]{1,0:T(8,128)} %bitcast.5, s32[1,32]{1,0:T(1,128)} %bitcast.7, f32[32,32,4096]{2,1,0:T(8,128)} %bitcast.4, f32[384]{0:T(512)} %occ.1, s32[1]{0:T(128)S(6)} %copy.8.slab_hbm, f32[1,2048]{1,0:T(1,128)} %bitcast.6), custom_call_target="tpu_custom_call" | custom-call | tf_op jit(solution)/shard_map/pallas_call | solution.py:468
  123.4 1.0 copy.9

commit v10 on v9

--- a/solution.py
+++ b/solution.py
@@ -266,14 +266,17 @@
     def whole(buf, k, c):
         return jnp.concatenate([buf[k, 2 * c].reshape(192, 128), buf[k, 2 * c + 1].reshape(192, 128)], axis=1)
 
-    def arrived(c):
-        for odd in range(2):
+    def landed(c, odds):
+        for odd in odds:
             i = 2 * c + odd
             step = 1 - 2 * odd
             got(rowbuf, y_send, y_recv, (y + step + 4) % 4, 1 - odd, i)
             got(colbuf, z_send, z_recv, (z + step + 4) % 4, 1 - odd, i)
             got(rowbuf, y_send, y_recv, (y + 2) % 4, 2, i)
             got(colbuf, z_send, z_recv, (z + 2) % 4, 2, i)
+
+    def arrived(c):
+        landed(c, (0, 1))
         for k in range(4):
             cols[k * 192:k * 192 + 192] = whole(colbuf, k, c)
         for m in range(6):
@@ -283,6 +286,18 @@
 
     def product_rows(c, k):
         acc[k] = acc[k] + dot3(split(whole(rowbuf, k, c)), (colh[...], coll[...]), NN)
+
+    def arrived_round(i):
+        landed(i // 2, (i % 2,))
+        for k in range(4):
+            cols[k * 192:k * 192 + 192, 0:128] = colbuf[k, i].reshape(192, 128)
+        for m in range(6):
+            high, low = split(cols[128 * m:128 * m + 128, 0:128].T)
+            colh[0:128, 128 * m:128 * m + 128] = high
+            coll[0:128, 128 * m:128 * m + 128] = low
+
+    def round_rows(i, k):
+        acc[k] = acc[k] + dot3(split(rowbuf[k, i].reshape(192, 128)), (colh[0:128], coll[0:128]), NN)
 
     def product_half(c, half):
         def part(k, _):
@@ -380,7 +395,14 @@
     product_half(6, 0)
     forward_z(15)
     product_half(6, 1)
-    arrived(7)
+    arrived_round(14)
+
+    def early(k, _):
+        round_rows(14, k)
+        return 0
+
+    lax.fori_loop(0, 4, early, 0)
+    arrived_round(15)
 
     mine = pl.ds(pl.multiple_of(core * 384, 128), 384)
     theirs = pl.ds(pl.multiple_of((1 - core) * 384, 128), 384)
@@ -391,7 +413,7 @@
         return copy(acc.at[k, :, theirs], exch.at[k], t_send.at[n], t_recv.at[n], mate)
 
     def finish(n):
-        product_rows(7, order[n])
+        round_rows(15, order[n])
         trade(n).start()
 
     def summed(n):

time: 125 us -> 126 us (level)
  no operation moved by 1% of the time
where the time goes in v10:
time: 126 us; the launch traced here: 124 us
  Pallas kernels  123 us (98%)
    pallas_call x1, Pallas kernels, amplitude_block(): pl.pallas_call(fused_kernel, out_shape=jax.ShapeDtypeStruct((192, 1536),...  123 us

profile of v10, /device:TPU:5, one launch (start us, length us, event | category | flops | bytes accessed | tf_op | source)
XLA Modules:
  0.0 124.4 jit_solution(18407585046458442011)
XLA Ops:
  0.7 122.7 %shard_map.64 = f32[192,1536]{1,0:T(8,128)S(1)} custom-call(f32[32,6144]{1,0:T(8,128)} %bitcast.5, s32[1,32]{1,0:T(1,128)} %bitcast.7, f32[32,32,4096]{2,1,0:T(8,128)} %bitcast.4, f32[384]{0:T(512)} %occ.1, s32[1]{0:T(128)S(6)} %copy.8.slab_hbm, f32[1,2048]{1,0:T(1,128)} %bitcast.6), custom_call_target="tpu_custom_call" | custom-call | tf_op jit(solution)/shard_map/pallas_call | solution.py:490
  123.4 1.0 copy.9
